TPU v7x, 128 devices: a whole 4x4x4 slice. The times are simulated.
128 devices in a mesh: section: 8 (over x_hi, z), rep: 16 (over x_lo, y, core).
Axes of the slice: x: 4 (x_hi: 2, x_lo: 2; x = x_hi * 2 + x_lo), y: 4, z: 4, core: 2. Of those that a mesh axis runs over, the one named last changes fastest.
Arguments:
- cache: bfloat16 [8, 8192, 3584], P('section', 'rep'), may hold values from -6 to 6
- payload: bfloat16 [8, 8192, 3584], P('section', 'rep'), may hold values from -6 to 6
- block_ids: int32 [8, 16, 2], P('section', 'rep'), may hold values from 0 to 3, as said below
- block_counts: int32 [8, 16], P('section', 'rep'), may hold values from 1 to 2, as said below
- block_scales: int32 [8, 16, 2], P('section', 'rep'), may hold values from 1024 to 8192
- refresh_ids: int32 [8, 16, 128], P('section', 'rep'), may hold values from 0 to 511, as said below
- refresh_counts: int32 [8, 16], P('section', 'rep'), may hold values from 1 to 128, as said below
- norm_gain: float32 [8, 3584], P('section'), may hold values from 0.5 to 1.5
- query_weight: bfloat16 [8, 3584, 3584], P('section', 'rep'), may hold values from -0.09375 to 0.09375
- query_bias: float32 [8, 3584], P('section'), may hold values from -3 to 3
- kv_weight: bfloat16 [8, 3584, 1024], P('section', 'rep'), may hold values from -0.09375 to 0.09375
- kv_bias: float32 [8, 1024], P('section'), may hold values from -3 to 3
Outputs:
- rebuilt: bfloat16 [8, 8192, 3584], P('section', 'rep')
- queries: bfloat16 [8, 8192, 3584], P('section', 'rep')
- keys_values: bfloat16 [8, 8192, 1024], P('section', 'rep')
Inputs may be any that keep to these rules, and one draw needn't show every extreme that they name: `block_ids`: for each section and relay the 2 entries are different block numbers; only the first block_counts entries are used. `block_counts`: in every section some relay lists exactly 2 blocks. `refresh_ids`: for each section and relay the entries are different local row numbers; only the first refresh_counts entries are used. `refresh_counts`: in every section some relay lists exactly 128 rows.
All inputs are finite; a program needn't handle non-finite values.
Results may differ from a plain program's by a relative error of at most 0.0052.
Values may be sent and summed in bfloat16 or wider, within the bound.
A program may use at most 256 MiB of HBM per device.

v0:
```python
import jax
import jax.numpy as jnp
from jax import lax
from jax.sharding import PartitionSpec as P

BLK = 128


EPSILON = 1e-06


def passed_along(block, axis, distance):
    devices = range(lax.axis_size(axis))
    route = [(i - distance, i) for i in devices if i - distance in devices]
    return lax.ppermute(block, axis, route)


def live_factor(got_ids, got_counts, got_scales):
    live = jnp.arange(got_ids.shape[0]) < got_counts
    return jnp.where(live, got_scales.astype(jnp.float32) / 4096.0, 0.0)


def live_rows(got_rows, got_rcounts, row_count):
    live = jnp.arange(got_rows.shape[0]) < got_rcounts
    return (got_rows[:, None] == jnp.arange(row_count)[None, :]) & live[:, None]


def body(
    cache,
    payload,
    block_ids,
    block_counts,
    block_scales,
    refresh_ids,
    refresh_counts,
    norm_gain,
    query_weight,
    query_bias,
    kv_weight,
    kv_bias,
):
    row_count = cache.shape[1]
    feature = cache.shape[2]
    blocks = row_count // BLK
    stored = cache[0].astype(jnp.float32)
    source = payload[0].reshape(blocks, BLK, feature)
    picked = jnp.take(source, block_ids[0, 0], axis=0)
    fresh = jnp.take(payload[0], refresh_ids[0, 0], axis=0)
    arrived = passed_along(
        (picked, fresh, block_ids, block_counts, block_scales, refresh_ids, refresh_counts),
        "section",
        1,
    )
    picked_in, fresh_in, got_ids, got_counts, got_scales, got_rows, got_rcounts = arrived
    factor = live_factor(got_ids[0, 0], got_counts[0, 0], got_scales[0, 0])
    scaled = (picked_in.astype(jnp.float32) * factor[:, None, None]).astype(jnp.bfloat16)
    select = (got_ids[0, 0][:, None] == jnp.arange(blocks)[None, :]).astype(jnp.bfloat16)
    delta = jnp.einsum("mn,mbd->nbd", select, scaled, preferred_element_type=jnp.float32).reshape(
        row_count, feature
    )
    matches = live_rows(got_rows[0, 0], got_rcounts[0, 0], row_count)
    spread = matches.astype(jnp.bfloat16)
    placed = jnp.einsum("kr,kd->rd", spread, fresh_in, preferred_element_type=jnp.float32)
    hit = jnp.any(matches, axis=0)
    mixed = jnp.where(hit[:, None], placed, stored + delta)
    rebuilt = mixed.astype(jnp.bfloat16)
    wide = rebuilt.astype(jnp.float32)
    scale_rows = lax.rsqrt(jnp.mean(wide * wide, axis=1, keepdims=True) + EPSILON)
    normed = (wide * scale_rows * norm_gain[0][None, :]).astype(jnp.bfloat16)

    def add_rows(piece):
        return jnp.dot(normed, piece[0], preferred_element_type=jnp.float32)

    query_sum = add_rows(lax.all_gather(query_weight, "rep", axis=1, tiled=True))
    kv_sum = add_rows(lax.all_gather(kv_weight, "rep", axis=1, tiled=True))
    queries = (query_sum + query_bias[0][None, :]).astype(jnp.bfloat16)
    keys_values = (kv_sum + kv_bias[0][None, :]).astype(jnp.bfloat16)
    return (rebuilt[None], queries[None], keys_values[None])


def solution(mesh):
    in_specs = (
        P("section", "rep", None),
        P("section", "rep", None),
        P("section", "rep", None),
        P("section", "rep"),
        P("section", "rep", None),
        P("section", "rep", None),
        P("section", "rep"),
        P("section", None),
        P("section", "rep", None),
        P("section", None),
        P("section", "rep", None),
        P("section", None),
    )
    out_specs = (P("section", "rep", None), P("section", "rep", None), P("section", "rep", None))
    return jax.shard_map(body, mesh=mesh, in_specs=in_specs, out_specs=out_specs, check_vma=False)
```

profile of v0, /device:TPU:121, one launch (start us, length us, event | category | flops | bytes accessed | tf_op | source)
XLA Modules:
  0.0 273.2 jit_solution(13666827860393578271)
XLA Ops:
  7.2 0.0 all-gather.5.cloned.1.call-start
  7.2 0.7 all-gather.5.cloned.1.call-update
  7.9 0.0 all-gather.3.cloned.1.call-start
  8.0 0.7 all-gather.3.cloned.1.call-update
  8.7 3.3 %collective-permute-start.3 = (s32[1,1,2]{2,1,0:T(1,128)}, s32[1,1,2]{2,1,0:T(1,128)S(1)}, u32[]{:S(2)}, u32[]{:S(2)}) collective-permute-start(s32[1,1,2]{2,1,0:T(1,128)} %param.14), channel_id=1, source_target_pairs={{0,16},{16,32},{32,48},{48,64},{64,80},{80,96},{96,112},{1,17},{17... | collective-permute-start | bytes 32 | tf_op jit(solution)/shard_map/ppermute | solution.py:15
  12.0 0.7 fusion.32
  12.6 0.0 copy-start.1
  12.7 0.0 copy-start.2
  12.7 2.7 gather_fusion.1
  15.4 1.5 broadcast_select_fusion
  16.9 3.5 %collective-permute-start.4 = (bf16[2,128,3584]{2,1,0:T(8,128)(2,1)}, bf16[2,128,3584]{2,1,0:T(8,128)(2,1)S(1)}, u32[]{:S(2)}, u32[]{:S(2)}) collective-permute-start(bf16[2,128,3584]{2,1,0:T(8,128)(2,1)} %broadcast_select_fusion), channel_id=1, source_target_pairs={{0,16},{16,32},{32,48},{48,64},{64,80},{80,96},{96,112},{1,17},{17... | collective-permute-start | bytes 5505032 | tf_op jit(solution)/shard_map/ppermute | solution.py:15
  20.4 3.5 %collective-permute-start.6 = (s32[1,1,2]{2,1,0:T(1,128)S(1)}, s32[1,1,2]{2,1,0:T(1,128)S(1)}, u32[]{:S(2)}, u32[]{:S(2)}) collective-permute-start(s32[1,1,2]{2,1,0:T(1,128)S(1)} %copy-done.4), channel_id=1, source_target_pairs={{0,16},{16,32},{32,48},{48,64},{64,80},{80,96},{96,112},{1,17},{17... | collective-permute-start | bytes 32 | tf_op jit(solution)/shard_map/ppermute | solution.py:15
  24.0 3.3 %collective-permute-start = (s32[1,1,128]{2,1,0:T(1,128)S(1)}, s32[1,1,128]{2,1,0:T(1,128)S(1)}, u32[]{:S(2)}, u32[]{:S(2)}) collective-permute-start(s32[1,1,128]{2,1,0:T(1,128)S(1)} %copy-done.5), channel_id=1, source_target_pairs={{0,16},{16,32},{32,48},{48,64},{64,80},{80,96},{96,112},{1,17},{17... | collective-permute-start | bytes 1544 | tf_op jit(solution)/shard_map/ppermute | solution.py:15
  27.3 1.9 collective-permute-start.1
  29.3 4.6 %gather_fusion = bf16[128,3584]{1,0:T(8,128)(2,1)S(1)} fusion(bf16[512,3584]{1,0:T(8,128)(2,1)} %bitcast.50, s32[1024]{0:T(1024)S(1)} %pad_clamp_fusion.1), kind=kCustom, calls=%fused_computation | custom fusion | bytes 1835520 | tf_op jit(solution)/shard_map/jit(_take)/gather | solution.py:48
  33.9 0.2 broadcast_select_fusion.1
  34.1 59.4 %collective-permute-done.1 = s32[1,1]{1,0:T(1,128)} collective-permute-done((s32[1,1]{1,0:T(1,128)}, s32[1,1]{1,0:T(1,128)}, u32[]{:S(2)}, u32[]{:S(2)}) %collective-permute-start.1) | collective-permute-done | bytes 36 | tf_op jit(solution)/shard_map/ppermute | solution.py:15
  93.4 7.6 %collective-permute-start.5 = (s32[1,1]{1,0:T(1,128)}, s32[1,1]{1,0:T(1,128)}, u32[]{:S(2)}, u32[]{:S(2)}) collective-permute-start(s32[1,1]{1,0:T(1,128)} %param.15), channel_id=1, source_target_pairs={{0,16},{16,32},{32,48},{48,64},{64,80},{80,96},{96,112},{1,17},{17... | collective-permute-start | bytes 20 | tf_op jit(solution)/shard_map/ppermute | solution.py:15
  101.1 0.6 iota_compare_fusion.1
  101.7 0.3 collective-permute-done.5
  101.9 7.3 %collective-permute-start.2 = (bf16[128,3584]{1,0:T(8,128)(2,1)S(1)}, bf16[128,3584]{1,0:T(8,128)(2,1)S(1)}, u32[]{:S(2)}, u32[]{:S(2)}) collective-permute-start(bf16[128,3584]{1,0:T(8,128)(2,1)S(1)} %broadcast_select_fusion.1), channel_id=1, source_target_pairs={{0,16},{16,32},{32,48},{48,64},{64,80},{80,96},{96,112},{1,17},{17... | collective-permute-start | bytes 2752520 | tf_op jit(solution)/shard_map/ppermute | solution.py:15
  109.3 0.6 compare_select_fusion.4
  109.9 0.1 fusion.25
  110.0 0.4 multiply_convert_fusion
  110.4 3.7 %fusion.14 = f32[4,128,3584]{2,0,1:T(4,128)S(1)} fusion(bf16[2,128,3584]{2,1,0:T(8,128)(2,1)S(1)} %multiply_convert_fusion, s32[2]{0:T(128)S(1)} %bitcast.54), kind=kOutput, calls=%fused_computation.18 | convolution fusion | flops 7340040 | bytes 9175048 | tf_op jit(solution)/shard_map/mn,mbd->nbd/dot_general | solution.py:58
  114.1 0.0 copy-start
  114.1 2.4 copy.19
  116.5 31.6 %collective-permute-done.2 = bf16[128,3584]{1,0:T(8,128)(2,1)S(1)} collective-permute-done((bf16[128,3584]{1,0:T(8,128)(2,1)S(1)}, bf16[128,3584]{1,0:T(8,128)(2,1)S(1)}, u32[]{:S(2)}, u32[]{:S(2)}) %collective-permute-start.2) | collective-permute-done | bytes 917536 | tf_op jit(solution)/shard_map/ppermute | solution.py:15
  148.1 4.0 %fusion.2 = (f32[512]{0:T(512)S(1)}, bf16[512,3584]{1,0:T(8,128)(2,1)}) fusion(f32[4,128,3584]{2,1,0:T(8,128)S(1)} %copy.19, bf16[1,512,3584]{2,1,0:T(8,128)(2,1)S(1)} %copy-done, bf16[128,3584]{1,0:T(8,128)(2,1)S(1)} %collective-permute-done.2, s32[128]{0:T(128)S(1)} %bitcast.53, pred[128]{0:T(512)(128)(4,1)S(1)} %iota_compare_fusion.1, ...), kind=kOutput, calls=%fused_computation.6 | convolution fusion | flops 482737664 | bytes 15600768 | tf_op jit(solution)/shard_map/kr,kd->rd/dot_general | solution.py:63
  152.1 9.4 %fusion.18 = bf16[1,512,1024]{2,1,0:T(8,128)(2,1)} fusion(bf16[1,3584,1024]{2,1,0:T(8,128)(2,1)} %all-gather.5.cloned.1.call-done, bf16[512,3584]{1,0:T(8,128)(2,1)} %get-tuple-element.4, f32[3584]{0:T(1024)S(1)} %reduce, f32[512]{0:T(512)S(1)} %add_rsqrt_fusion, f32[1024]{0:T(1024)S(1)} %bitcast.55), kind=kOutput, calls=%fused_computation.21 | convolution fusion | flops 3766484992 | bytes 12079104 | tf_op jit(solution)/shard_map/dot_general | solution.py:72
  161.5 84.1 %all-gather.3.cloned.1.call-done = bf16[1,3584,3584]{2,1,0:T(8,128)(2,1)} async-done(((bf16[1,224,3584]{2,1,0:T(8,128)(2,1)}), bf16[1,3584,3584]{2,1,0:T(8,128)(2,1)}) %all-gather.3.cloned.1.call-update) | async-done | bytes 25690128 | tf_op jit(solution)/shard_map/all_gather | solution.py:74
  245.6 20.8 %fusion.11 = bf16[1,512,3584]{2,1,0:T(8,128)(2,1)} fusion(bf16[1,3584,3584]{2,1,0:T(8,128)(2,1)} %all-gather.3.cloned.1.call-done, f32[3584]{0:T(1024)S(1)} %reduce.1, bf16[512,3584]{1,0:T(8,128)(2,1)} %get-tuple-element.4, f32[3584]{0:T(1024)S(1)} %reduce, f32[512]{0:T(512)S(1)} %add_rsqrt_fusion), kind=kOutput, calls=%fused_computation.15 | convolution fusion | flops 13164347392 | bytes 33060864 | tf_op jit(solution)/shard_map/dot_general | solution.py:72
  (24 shorter events, 0.2 us)
Async XLA Ops:
  7.2 8.2 %copy-start.6 = (s32[1,1,2]{2,1,0:T(1,128)S(1)}, s32[1,1,2]{2,1,0:T(1,128)}, u32[]{:S(2)}) copy-start(s32[1,1,2]{2,1,0:T(1,128)} %param.14) | copy-start | bytes 28
  7.2 144.9 %all-gather.5.cloned.1.call-start = ((), (), s32[]{:S(2)}) async-start(), calls=%async_computation.1 | async-start | bytes 7798784 | tf_op jit(solution)/shard_map/all_gather | solution.py:75
  7.9 237.7 %all-gather.3.cloned.1.call-start = ((), (), s32[]{:S(2)}) async-start(), calls=%async_computation | async-start | bytes 27295744 | tf_op jit(solution)/shard_map/all_gather | solution.py:74
  8.7 101.8 %collective-permute-start.3 = (s32[1,1,2]{2,1,0:T(1,128)}, s32[1,1,2]{2,1,0:T(1,128)S(1)}, u32[]{:S(2)}, u32[]{:S(2)}) collective-permute-start(s32[1,1,2]{2,1,0:T(1,128)} %param.14), channel_id=1, source_target_pairs={{0,16},{16,32},{32,48},{48,64},{64,80},{80,96},{96,112},{1,17},{17... | collective-permute-start | bytes 32 | tf_op jit(solution)/shard_map/ppermute | solution.py:15
  12.6 7.8 %copy-start.4 = (s32[1,1,2]{2,1,0:T(1,128)S(1)}, s32[1,1,2]{2,1,0:T(1,128)}, u32[]{:S(2)}) copy-start(s32[1,1,2]{2,1,0:T(1,128)} %param.16) | copy-start | bytes 28
  12.6 11.4 %copy-start.5 = (s32[1,1,128]{2,1,0:T(1,128)S(1)}, s32[1,1,128]{2,1,0:T(1,128)}, u32[]{:S(2)}) copy-start(s32[1,1,128]{2,1,0:T(1,128)} %param.17) | copy-start | bytes 1540
  12.6 16.6 %copy-start.1 = (f32[1,3584]{1,0:T(1,128)S(1)}, f32[1,3584]{1,0:T(1,128)}, u32[]{:S(2)}) copy-start(f32[1,3584]{1,0:T(1,128)} %param.21) | copy-start | bytes 43012
  12.7 16.6 %copy-start.2 = (f32[1,3584]{1,0:T(1,128)S(1)}, f32[1,3584]{1,0:T(1,128)}, u32[]{:S(2)}) copy-start(f32[1,3584]{1,0:T(1,128)} %param.19) | copy-start | bytes 43012
  16.9 93.1 %collective-permute-start.4 = (bf16[2,128,3584]{2,1,0:T(8,128)(2,1)}, bf16[2,128,3584]{2,1,0:T(8,128)(2,1)S(1)}, u32[]{:S(2)}, u32[]{:S(2)}) collective-permute-start(bf16[2,128,3584]{2,1,0:T(8,128)(2,1)} %broadcast_select_fusion), channel_id=1, source_target_pairs={{0,16},{16,32},{32,48},{48,64},{64,80},{80,96},{96,112},{1,17},{17... | collective-permute-start | bytes 5505032 | tf_op jit(solution)/shard_map/ppermute | solution.py:15
  20.4 88.8 %collective-permute-start.6 = (s32[1,1,2]{2,1,0:T(1,128)S(1)}, s32[1,1,2]{2,1,0:T(1,128)S(1)}, u32[]{:S(2)}, u32[]{:S(2)}) collective-permute-start(s32[1,1,2]{2,1,0:T(1,128)S(1)} %copy-done.4), channel_id=1, source_target_pairs={{0,16},{16,32},{32,48},{48,64},{64,80},{80,96},{96,112},{1,17},{17... | collective-permute-start | bytes 32 | tf_op jit(solution)/shard_map/ppermute | solution.py:15
  24.0 85.9 %collective-permute-start = (s32[1,1,128]{2,1,0:T(1,128)S(1)}, s32[1,1,128]{2,1,0:T(1,128)S(1)}, u32[]{:S(2)}, u32[]{:S(2)}) collective-permute-start(s32[1,1,128]{2,1,0:T(1,128)S(1)} %copy-done.5), channel_id=1, source_target_pairs={{0,16},{16,32},{32,48},{48,64},{64,80},{80,96},{96,112},{1,17},{17... | collective-permute-start | bytes 1544 | tf_op jit(solution)/shard_map/ppermute | solution.py:15
  27.3 66.2 %collective-permute-start.1 = (s32[1,1]{1,0:T(1,128)}, s32[1,1]{1,0:T(1,128)}, u32[]{:S(2)}, u32[]{:S(2)}) collective-permute-start(s32[1,1]{1,0:T(1,128)} %param.18), channel_id=1, source_target_pairs={{0,16},{16,32},{32,48},{48,64},{64,80},{80,96},{96,112},{1,17},{17... | collective-permute-start | bytes 20 | tf_op jit(solution)/shard_map/ppermute | solution.py:15
  93.4 8.5 %collective-permute-start.5 = (s32[1,1]{1,0:T(1,128)}, s32[1,1]{1,0:T(1,128)}, u32[]{:S(2)}, u32[]{:S(2)}) collective-permute-start(s32[1,1]{1,0:T(1,128)} %param.15), channel_id=1, source_target_pairs={{0,16},{16,32},{32,48},{48,64},{64,80},{80,96},{96,112},{1,17},{17... | collective-permute-start | bytes 20 | tf_op jit(solution)/shard_map/ppermute | solution.py:15
  101.9 46.2 %collective-permute-start.2 = (bf16[128,3584]{1,0:T(8,128)(2,1)S(1)}, bf16[128,3584]{1,0:T(8,128)(2,1)S(1)}, u32[]{:S(2)}, u32[]{:S(2)}) collective-permute-start(bf16[128,3584]{1,0:T(8,128)(2,1)S(1)} %broadcast_select_fusion.1), channel_id=1, source_target_pairs={{0,16},{16,32},{32,48},{48,64},{64,80},{80,96},{96,112},{1,17},{17... | collective-permute-start | bytes 2752520 | tf_op jit(solution)/shard_map/ppermute | solution.py:15
  114.1 34.0 %copy-start = (bf16[1,512,3584]{2,1,0:T(8,128)(2,1)S(1)}, bf16[1,512,3584]{2,1,0:T(8,128)(2,1)}, u32[]{:S(2)}) copy-start(bf16[1,512,3584]{2,1,0:T(8,128)(2,1)} %param.12) | copy-start | bytes 11010052
  116.5 35.6 %copy-start.3 = (f32[1,1024]{1,0:T(1,128)S(1)}, f32[1,1024]{1,0:T(1,128)}, u32[]{:S(2)}) copy-start(f32[1,1024]{1,0:T(1,128)} %param.23) | copy-start | bytes 12292
Sparse Core Ops, SparseCore 0:
  9.7 82.5 all-gather.4
  94.0 151.5 all-gather.2
where the time goes:
time: 274 us; the launch traced here: 273 us
  waiting for transfers between devices  177 us (65%)
  matrix products  37.8 us (14%)
  starting transfers between devices  30.6 us (11%)
  between operations  14.3 us (5%)
  local copies, waits for them, and re-layouts  9.68 us (4%)
  other arithmetic  4.08 us (1%)
    ppermute x7, waiting for transfers between devices, passed_along(): return lax.ppermute(block, axis, route)  91.2 us
    all_gather x1, waiting for transfers between devices, body(): lax.all_gather(query_weight, 'rep', axis=1, tiled=True)  84.1 us
    ppermute x7, starting transfers between devices, passed_along(): return lax.ppermute(block, axis, route)  30.5 us
    dot_general x2, matrix products, add_rows(): return jnp.dot(normed, piece[0], preferred_element_type=jnp.float32)  30.2 us
  transfers between devices with their start and end apart: 9, of which 4 were waited for; matrix products, arithmetic and copies ran while one was open for 11% of the time, Pallas kernels for 0%

commit v1 on v0

v1 whole, which is shorter than its diff:
```python
import functools

import jax
import jax.numpy as jnp
from jax import lax
from jax.experimental import pallas as pl
from jax.experimental.pallas import tpu as pltpu
from jax.sharding import PartitionSpec as P

EPSILON = 1e-06
BLK = 128
COLS = 256
GRP = 3
MESH = pl.DeviceIdType.MESH

YM, YP, XP, SIB = 0, 1, 2, 3
Y2B, Y2C, Y2A = 4, 5, 6
XYM_BC, XYP_BC, XYP_A, XYM_A = 7, 8, 9, 10
XY2B, XY2C, XY2A = 11, 12, 13
D_YM, D_YP, D_XP, D_Y2, D_XYM, D_XYP, D_XY2 = 14, 15, 16, 17, 18, 19, 20
CLASSES = 21


def kernel(
    cache, payload, meta, gain, q_w, q_b, kv_w, kv_b,
    rebuilt_out, qkv_out,
    wbuf, pay, held, normed, outbuf, relay, meta_in, bias,
    ld_sem, cache_sem, send, recv, pay_send, pay_recv, meta_send, meta_recv,
    relay_send, relay_recv, reb_sem, out_sem,
):
    sec = lax.axis_index("section")
    me = lax.axis_index("rep")
    depth = q_w.shape[0]
    q_blocks = q_w.shape[1] // COLS
    blocks = q_blocks + kv_w.shape[1] // COLS
    groups = blocks // GRP
    row_blocks = payload.shape[0] // BLK

    x, y, core = me // 8, (me // 2) % 4, me % 2

    def rank(dx, dy):
        return ((x + dx) % 2) * 8 + ((y + dy) % 4) * 2 + core

    ym, yp, y2 = rank(0, 3), rank(0, 1), rank(0, 2)
    xp, xym, xyp, xy2 = rank(1, 0), rank(1, 3), rank(1, 1), rank(1, 2)
    other = me + 1 - 2 * core

    def twin(r):
        return r + 1 - 2 * core

    def region(r, first, count):
        rows = pl.ds(pl.multiple_of(r * depth, 32), depth)
        return wbuf.at[pl.ds(first, count), rows, :]

    def remote(ref, cls, g, to):
        return pltpu.make_async_remote_copy(
            src_ref=ref, dst_ref=ref, send_sem=send.at[cls, g], recv_sem=recv.at[cls, g],
            device_id=(sec, to), device_id_type=MESH,
        )

    sent = []

    def push(r, first, count, cls, g, to):
        copy = remote(region(r, first, count), cls, g, to)
        copy.start()
        sent.append(copy)

    def arrive(r, first, count, cls, g):
        remote(region(r, first, count), cls, g, other).wait_recv()

    loads = []
    for j in range(blocks):
        if j < q_blocks:
            src = q_w.at[:, pl.ds(j * COLS, COLS)]
        else:
            src = kv_w.at[:, pl.ds((j - q_blocks) * COLS, COLS)]
        rows = pl.ds(pl.multiple_of(me * depth, 32), depth)
        copy = pltpu.make_async_copy(src, wbuf.at[j, rows, :], ld_sem.at[j])
        copy.start()
        loads.append(copy)

    def block(ref, b):
        return ref.at[pl.ds(b * BLK, BLK), :]

    def pay_copy(src, dst, b, to_sec, to_rep, send_sem, recv_sem):
        return pltpu.make_async_remote_copy(
            src_ref=src, dst_ref=dst, send_sem=send_sem, recv_sem=recv_sem,
            device_id=(to_sec, to_rep), device_id_type=MESH,
        )

    last = lax.axis_size("section") - 1
    half = (last + 1) // 2
    via = (half - 1, last, half, 0)

    def direct(b):
        return pay_copy(block(payload, b), block(pay, b), b, lax.rem(sec + 1, last + 1), me, pay_send.at[b], pay_recv.at[b])

    def first_hop(b):
        return pay_copy(block(payload, b), relay, b, via[b], xp, pay_send.at[b], relay_recv)

    def second_hop(b):
        return pay_copy(relay, block(pay, b), b, half, xp, relay_send, pay_recv.at[b])

    def meta_copy():
        return pay_copy(meta, meta_in, 0, lax.rem(sec + 1, last + 1), me, meta_send, meta_recv)

    @pl.when(sec != last)
    def _():
        meta_copy().start()

    @pl.when(sec == half - 1)
    def _():
        for b in range(row_blocks):
            first_hop(b).start()

    @pl.when((sec != half - 1) & (sec != last))
    def _():
        for b in range(row_blocks):
            direct(b).start()

    fill_meta = pltpu.make_async_copy(meta, meta_in, meta_recv)

    def fill(b):
        return pltpu.make_async_copy(block(payload, b), block(pay, b), pay_recv.at[b])

    @pl.when(sec == 0)
    def _():
        fill_meta.start()
        for b in range(row_blocks):
            fill(b).start()

    load_cache = pltpu.make_async_copy(cache, held, cache_sem)
    load_cache.start()

    for g in range(groups):
        for j in range(g * GRP, (g + 1) * GRP):
            loads[j].wait()
        push(me, g * GRP, GRP, XP, g, xp)
        push(me, g * GRP, GRP, YM, g, yp)
        push(me, g * GRP, GRP, YP, g, ym)
        push(me, g * GRP, GRP, SIB, g, other)

    bias[:, : q_w.shape[1]] = q_b[...]
    bias[:, q_w.shape[1] :] = kv_b[...]

    def level1(g):
        a = g * GRP
        arrive(ym, a, GRP, YM, g)
        push(ym, a + 1, 1, Y2B, g, yp)
        if g % 2 == 0:
            push(ym, a, 1, Y2A, g, yp)
        push(ym, a, 1, XYM_A, g, xp)
        arrive(yp, a, GRP, YP, g)
        push(yp, a + 2, 1, Y2C, g, ym)
        if g % 2 == 1:
            push(yp, a, 1, Y2A, g, ym)
        push(yp, a, 1, XYP_A, g, xp)
        arrive(xp, a, GRP, XP, g)
        push(xp, a + 1, 2, XYM_BC, g, yp)
        push(xp, a + 1, 2, XYP_BC, g, ym)
        push(ym, a, GRP, D_YM, g, other)
        push(yp, a, GRP, D_YP, g, other)
        push(xp, a, GRP, D_XP, g, other)

    def level2(g):
        a = g * GRP
        arrive(xym, a + 1, 2, XYM_BC, g)
        push(xym, a + 1, 1, XY2B, g, yp)
        arrive(xyp, a + 1, 2, XYP_BC, g)
        push(xyp, a + 2, 1, XY2C, g, ym)
        arrive(y2, a, 1, Y2A, g)
        push(y2, a, 1, XY2A, g, xp)
        arrive(y2, a + 1, 1, Y2B, g)
        arrive(y2, a + 2, 1, Y2C, g)
        push(y2, a, GRP, D_Y2, g, other)
        arrive(xym, a, 1, XYM_A, g)
        push(xym, a, GRP, D_XYM, g, other)
        arrive(xyp, a, 1, XYP_A, g)
        push(xyp, a, GRP, D_XYP, g, other)

    def level3(g):
        a = g * GRP
        arrive(xy2, a + 1, 1, XY2B, g)
        arrive(xy2, a + 2, 1, XY2C, g)
        arrive(xy2, a, 1, XY2A, g)
        push(xy2, a, GRP, D_XY2, g, other)

    def relay_step():
        for b in range(row_blocks):
            @pl.when(sec == via[b])
            def _():
                first_hop(b).wait_recv()
                second_hop(b).start()

    valid = sec > 0
    rebuilt_copies = []

    def rebuild(b):
        @pl.when(sec != 0)
        def _():
            direct(b).wait_recv()

        @pl.when(sec == 0)
        def _():
            fill(b).wait()

        lists = meta_in[...]
        lane = lax.broadcasted_iota(jnp.int32, (1, BLK), 1)
        ids = jnp.where((lane < lists[1:2, :]) & valid, lists[0:1, :], -1)
        listed = (lane < lists[4:5, :]) & (lists[2:3, :] == b) & valid
        factor = jnp.sum(jnp.where(listed, lists[3:4, :].astype(jnp.float32) / 4096.0, 0.0), axis=1, keepdims=True)
        strip = 16

        def one(i, carry):
            start = pl.multiple_of(b * BLK + i * strip, strip)
            rows = pl.ds(start, strip)
            number = lax.broadcasted_iota(jnp.int32, (strip, BLK), 0) + start
            hit = jnp.max(jnp.where(number == ids, 1.0, 0.0), axis=1, keepdims=True) > 0.0
            came = pay[rows, :].astype(jnp.float32)
            delta = (came * factor).astype(jnp.bfloat16).astype(jnp.float32)
            mixed = jnp.where(hit, came, held[rows, :].astype(jnp.float32) + delta).astype(jnp.bfloat16)
            held[rows, :] = mixed
            wide = mixed.astype(jnp.float32)
            scale = lax.rsqrt(jnp.mean(wide * wide, axis=1, keepdims=True) + EPSILON)
            normed[rows, :] = (wide * scale * gain[...]).astype(jnp.bfloat16)
            return carry

        lax.fori_loop(0, BLK // strip, one, 0)
        copy = pltpu.make_async_copy(block(held, b), block(rebuilt_out, b), reb_sem.at[b])
        copy.start()
        rebuilt_copies.append(copy)

    def out_copy(j):
        cols = pl.ds(pl.multiple_of(j * COLS, COLS), COLS)
        return pltpu.make_async_copy(outbuf.at[j], qkv_out.at[:, cols], out_sem.at[j])

    def compute(g):
        a = g * GRP
        for r, cls in ((me, SIB), (ym, D_YM), (yp, D_YP), (xp, D_XP), (y2, D_Y2), (xym, D_XYM), (xyp, D_XYP), (xy2, D_XY2)):
            arrive(twin(r), a, GRP, cls, g)

        def one(j, carry):
            total = jnp.dot(normed[...], wbuf[j], preferred_element_type=jnp.float32)
            cols = pl.ds(pl.multiple_of(j * COLS, COLS), COLS)
            outbuf[j] = (total + bias[:, cols]).astype(jnp.bfloat16)
            out_copy(j).start()
            return carry

        lax.fori_loop(a, a + GRP, one, 0)

    level1(0)
    level1(1)
    load_cache.wait()

    @pl.when(sec != 0)
    def _():
        meta_copy().wait_recv()

    @pl.when(sec == 0)
    def _():
        fill_meta.wait()

    relay_step()
    rebuild(0)
    rebuild(1)
    level2(0)
    level1(2)
    rebuild(2)
    level2(1)
    level3(0)
    level1(3)
    level2(2)
    level3(1)
    level1(4)
    rebuild(3)
    level2(3)
    level3(2)
    level1(5)
    compute(0)
    compute(1)
    level2(4)
    level3(3)
    compute(2)
    compute(3)
    level2(5)
    level3(4)
    compute(4)
    level3(5)
    compute(5)

    for copy in sent:
        copy.wait_send()
    for copy in rebuilt_copies:
        copy.wait()
    for j in range(blocks):
        out_copy(j).wait()

    @pl.when(sec != last)
    def _():
        meta_copy().wait_send()
        for b in range(row_blocks):
            direct(b).wait_send()

    for b in range(row_blocks):
        @pl.when(sec == via[b])
        def _():
            second_hop(b).wait_send()


def body(
    cache, payload, block_ids, block_counts, block_scales, refresh_ids, refresh_counts,
    norm_gain, query_weight, query_bias, kv_weight, kv_bias,
):
    rows, feature = cache.shape[1:]
    depth, q_cols = query_weight.shape[1:]
    kv_cols = kv_weight.shape[2]
    blocks = (q_cols + kv_cols) // COLS
    groups = blocks // GRP
    row_blocks = rows // BLK

    def lanes(v):
        return jnp.pad(v.reshape(1, -1), ((0, 0), (0, BLK - v.size)))

    meta = jnp.concatenate(
        [
            lanes(refresh_ids[0, 0]),
            jnp.broadcast_to(refresh_counts[0, 0], (1, BLK)),
            lanes(block_ids[0, 0]),
            lanes(block_scales[0, 0]),
            jnp.broadcast_to(block_counts[0, 0], (1, BLK)),
            jnp.zeros((3, BLK), jnp.int32),
        ],
        axis=0,
    )
    anywhere = pl.BlockSpec(memory_space=pl.ANY)
    vmem = pl.BlockSpec(memory_space=pltpu.VMEM)
    dma = pltpu.SemaphoreType.DMA
    rebuilt, qkv = pl.pallas_call(
        kernel,
        out_shape=(
            jax.ShapeDtypeStruct((rows, feature), jnp.bfloat16),
            jax.ShapeDtypeStruct((rows, q_cols + kv_cols), jnp.bfloat16),
        ),
        in_specs=[anywhere, anywhere, anywhere, vmem, anywhere, vmem, anywhere, vmem],
        out_specs=(anywhere, anywhere),
        scratch_shapes=[
            pltpu.VMEM((blocks, feature, COLS), jnp.bfloat16),
            pltpu.VMEM((rows, feature), jnp.bfloat16),
            pltpu.VMEM((rows, feature), jnp.bfloat16),
            pltpu.VMEM((rows, feature), jnp.bfloat16),
            pltpu.VMEM((blocks, rows, COLS), jnp.bfloat16),
            pltpu.VMEM((BLK, feature), jnp.bfloat16),
            pltpu.VMEM((8, BLK), jnp.int32),
            pltpu.VMEM((1, q_cols + kv_cols), jnp.float32),
            dma((blocks,)),
            dma,
            dma((CLASSES, groups)),
            dma((CLASSES, groups)),
            dma((row_blocks,)),
            dma((row_blocks,)),
            dma,
            dma,
            dma,
            dma,
            dma((row_blocks,)),
            dma((blocks,)),
        ],
        compiler_params=pltpu.CompilerParams(has_side_effects=True, vmem_limit_bytes=64 * 1024 * 1024 - 65536),
        name="boundary",
    )(cache[0], payload[0], meta, norm_gain, query_weight[0], query_bias, kv_weight[0], kv_bias)
    return rebuilt[None], qkv[None, :, :q_cols], qkv[None, :, q_cols:]


def solution(mesh):
    in_specs = (
        P("section", "rep", None),
        P("section", "rep", None),
        P("section", "rep", None),
        P("section", "rep"),
        P("section", "rep", None),
        P("section", "rep", None),
        P("section", "rep"),
        P("section", None),
        P("section", "rep", None),
        P("section", None),
        P("section", "rep", None),
        P("section", None),
    )
    out_specs = (P("section", "rep", None), P("section", "rep", None), P("section", "rep", None))
    return jax.shard_map(body, mesh=mesh, in_specs=in_specs, out_specs=out_specs, check_vma=False)
```

time: 274 us -> 188 us (0.69)
  the two profiles are of different devices: /device:TPU:121 before, /device:TPU:6 now
where the time goes in v1:
time: 188 us
  Pallas kernels  175 us (93%)
  local copies, waits for them, and re-layouts  11 us (6%)
  between operations  1.95 us (1%)
    pallas_call x1, Pallas kernels, body(): pl.pallas_call(kernel, out_shape=(jax.ShapeDtypeStruct((rows, feature), j...  175 us
    broadcast_in_dim x2, local copies, waits for them, and re-layouts, body(): return (rebuilt[None], qkv[None, :, :q_cols], qkv[None, :, q_cols:])  6.52 us

profile of v1, /device:TPU:6, one launch (start us, length us, event | category | flops | bytes accessed | tf_op | source)
XLA Modules:
  0.0 188.2 jit_solution(15814097986288863347)
XLA Ops:
  1.9 0.7 pad.7
  2.6 0.7 pad.8
  3.3 1.3 concatenate.3.meta
  4.5 175.3 %boundary.1 = (bf16[512,3584]{1,0:T(8,128)(2,1)}, bf16[512,4608]{1,0:T(8,128)(2,1)}) custom-call(bf16[512,3584]{1,0:T(8,128)(2,1)} %bitcast.17, bf16[512,3584]{1,0:T(8,128)(2,1)} %bitcast.18, s32[8,128]{1,0:T(8,128)} %concatenate.3.meta, f32[1,3584]{1,0:T(1,128)} %gain.1, bf16[224,3584]{1,0:T(8,128)(2,1)} %bitcast.19, f32[1,3584]{1,0:T(1,128)} %q_b.1, ...), custom_call_target="tpu_custom_call" | custom-call | tf_op jit(solution)/shard_map/boundary/pallas_call | solution.py:338
  179.8 2.3 %slice_bitcast_fusion.1 = bf16[1,512,1024]{2,1,0:T(8,128)(2,1)} fusion(bf16[512,4608]{1,0:T(8,128)(2,1)} %get-tuple-element.6), kind=kLoop, calls=%fused_computation.1 | loop fusion | bytes 2097152 | tf_op jit(solution)/shard_map/broadcast_in_dim | solution.py:371
  182.1 0.0 copy-start
  182.1 4.3 %slice_bitcast_fusion = bf16[1,512,3584]{2,1,0:T(8,128)(2,1)} fusion(bf16[512,4608]{1,0:T(8,128)(2,1)} %get-tuple-element.6), kind=kLoop, calls=%fused_computation | loop fusion | bytes 7340032 | tf_op jit(solution)/shard_map/broadcast_in_dim | solution.py:371
  186.4 0.0 copy-done
  186.4 1.8 copy.18
  (3 shorter events, 0.0 us)
Async XLA Ops:
  182.1 4.3 %copy-start = (bf16[512,3584]{1,0:T(8,128)(2,1)S(1)}, bf16[512,3584]{1,0:T(8,128)(2,1)}, u32[]{:S(2)}) copy-start(bf16[512,3584]{1,0:T(8,128)(2,1)} %get-tuple-element.5) | copy-start | bytes 11010052

commit v2 on v1

--- a/solution.py
+++ b/solution.py
@@ -22,11 +22,11 @@
 
 
 def kernel(
-    cache, payload, meta, gain, q_w, q_b, kv_w, kv_b,
-    rebuilt_out, qkv_out,
-    wbuf, pay, held, normed, outbuf, relay, meta_in, bias,
+    cache, payload, ids, counts, scales, refresh_ids, refresh_counts, gain, q_w, q_b, kv_w, kv_b,
+    rebuilt_out, q_out, kv_out,
+    wbuf, pay, held, normed, outbuf, relay, relay_two, meta, meta_in, bias,
     ld_sem, cache_sem, send, recv, pay_send, pay_recv, meta_send, meta_recv,
-    relay_send, relay_recv, reb_sem, out_sem,
+    relay_send, relay_recv, two_send, two_recv, reb_sem, out_sem,
 ):
     sec = lax.axis_index("section")
     me = lax.axis_index("rep")
@@ -79,30 +79,84 @@
         copy.start()
         loads.append(copy)
 
+    lane = lax.broadcasted_iota(jnp.int32, (1, BLK), 1)
+
+    def two(v):
+        return jnp.where(lane == 0, v[:, 0:1], v[:, 1:2])
+
+    meta[0:1, :] = refresh_ids[...]
+    meta[1:2, :] = jnp.broadcast_to(refresh_counts[...], (1, BLK))
+    meta[2:3, :] = two(ids[...])
+    meta[3:4, :] = two(scales[...])
+    meta[4:5, :] = jnp.broadcast_to(counts[...], (1, BLK))
+    meta[5:8, :] = jnp.zeros((3, BLK), jnp.int32)
+
+    load_cache = pltpu.make_async_copy(cache, held, cache_sem)
+    load_cache.start()
+
+    last = lax.axis_size("section") - 1
+    half = (last + 1) // 2
+    barrier = pltpu.get_barrier_semaphore()
+
+    def greet(to_sec, to_rep):
+        pl.semaphore_signal(barrier, inc=1, device_id=(to_sec, to_rep), device_id_type=MESH)
+
+    for r in (ym, yp, xp, other):
+        greet(sec, r)
+    expected = 4
+    pairs = [(s, s + 1, me) for s in range(last)]
+    pairs += [(0, half - 1, me), (half - 1, last, xp), (half - 1, half, xp), (half, last, xp), (0, half, xp)]
+    for one, two, r in pairs:
+        @pl.when(sec == one)
+        def _():
+            greet(two, r)
+
+        @pl.when(sec == two)
+        def _():
+            greet(one, r)
+
+        expected = expected + jnp.where((sec == one) | (sec == two), 1, 0)
+    pl.semaphore_wait(barrier, expected)
+
     def block(ref, b):
         return ref.at[pl.ds(b * BLK, BLK), :]
 
-    def pay_copy(src, dst, b, to_sec, to_rep, send_sem, recv_sem):
+    def pay_copy(src, dst, to_sec, to_rep, send_sem, recv_sem):
         return pltpu.make_async_remote_copy(
             src_ref=src, dst_ref=dst, send_sem=send_sem, recv_sem=recv_sem,
             device_id=(to_sec, to_rep), device_id_type=MESH,
         )
 
-    last = lax.axis_size("section") - 1
-    half = (last + 1) // 2
-    via = (half - 1, last, half, 0)
+    following = lax.rem(sec + 1, last + 1)
+    via = (half, half - 1, last, 0)
 
     def direct(b):
-        return pay_copy(block(payload, b), block(pay, b), b, lax.rem(sec + 1, last + 1), me, pay_send.at[b], pay_recv.at[b])
+        return pay_copy(block(payload, b), block(pay, b), following, me, pay_send.at[b], pay_recv.at[b])
 
     def first_hop(b):
-        return pay_copy(block(payload, b), relay, b, via[b], xp, pay_send.at[b], relay_recv)
-
-    def second_hop(b):
-        return pay_copy(relay, block(pay, b), b, half, xp, relay_send, pay_recv.at[b])
+        return pay_copy(block(payload, b), relay, via[b], xp if via[b] else me, pay_send.at[b], relay_recv)
+
+    def middle_hop():
+        return pay_copy(relay, relay_two, 0, xp, relay_send, two_recv)
+
+    def last_hop(b):
+        src, sem = (relay, relay_send) if via[b] else (relay_two, two_send)
+        return pay_copy(src, block(pay, b), half, xp, sem, pay_recv.at[b])
+
+    def relay_step(b):
+        @pl.when(sec == via[b])
+        def _():
+            first_hop(b).wait_recv()
+            (last_hop(b) if via[b] else middle_hop()).start()
+
+    def relay_end(b):
+        @pl.when(sec == 0)
+        def _():
+            middle_hop().wait_recv()
+            last_hop(b).start()
 
     def meta_copy():
-        return pay_copy(meta, meta_in, 0, lax.rem(sec + 1, last + 1), me, meta_send, meta_recv)
+        return pay_copy(meta, meta_in, following, me, meta_send, meta_recv)
 
     @pl.when(sec != last)
     def _():
@@ -110,7 +164,7 @@
 
     @pl.when(sec == half - 1)
     def _():
-        for b in range(row_blocks):
+        for b in (0, 2, 3):
             first_hop(b).start()
 
     @pl.when((sec != half - 1) & (sec != last))
@@ -118,26 +172,30 @@
         for b in range(row_blocks):
             direct(b).start()
 
-    fill_meta = pltpu.make_async_copy(meta, meta_in, meta_recv)
-
     def fill(b):
         return pltpu.make_async_copy(block(payload, b), block(pay, b), pay_recv.at[b])
 
     @pl.when(sec == 0)
     def _():
-        fill_meta.start()
+        meta_in[...] = jnp.zeros((8, BLK), jnp.int32)
         for b in range(row_blocks):
             fill(b).start()
 
-    load_cache = pltpu.make_async_copy(cache, held, cache_sem)
-    load_cache.start()
+    def own_x(g):
+        push(me, g * GRP, GRP, XP, g, xp)
 
     for g in range(groups):
         for j in range(g * GRP, (g + 1) * GRP):
             loads[j].wait()
-        push(me, g * GRP, GRP, XP, g, xp)
         push(me, g * GRP, GRP, YM, g, yp)
         push(me, g * GRP, GRP, YP, g, ym)
+        if g < groups // 2:
+            own_x(g)
+        if g == 1:
+            @pl.when(sec == half - 1)
+            def _():
+                first_hop(1).start()
+
         push(me, g * GRP, GRP, SIB, g, other)
 
     bias[:, : q_w.shape[1]] = q_b[...]
@@ -145,22 +203,22 @@
 
     def level1(g):
         a = g * GRP
+        arrive(xp, a, GRP, XP, g)
+        push(xp, a + 1, 2, XYM_BC, g, yp)
+        push(xp, a + 1, 2, XYP_BC, g, ym)
+        push(xp, a, GRP, D_XP, g, other)
         arrive(ym, a, GRP, YM, g)
         push(ym, a + 1, 1, Y2B, g, yp)
         if g % 2 == 0:
             push(ym, a, 1, Y2A, g, yp)
         push(ym, a, 1, XYM_A, g, xp)
+        push(ym, a, GRP, D_YM, g, other)
         arrive(yp, a, GRP, YP, g)
         push(yp, a + 2, 1, Y2C, g, ym)
         if g % 2 == 1:
             push(yp, a, 1, Y2A, g, ym)
         push(yp, a, 1, XYP_A, g, xp)
-        arrive(xp, a, GRP, XP, g)
-        push(xp, a + 1, 2, XYM_BC, g, yp)
-        push(xp, a + 1, 2, XYP_BC, g, ym)
-        push(ym, a, GRP, D_YM, g, other)
         push(yp, a, GRP, D_YP, g, other)
-        push(xp, a, GRP, D_XP, g, other)
 
     def level2(g):
         a = g * GRP
@@ -185,13 +243,6 @@
         arrive(xy2, a, 1, XY2A, g)
         push(xy2, a, GRP, D_XY2, g, other)
 
-    def relay_step():
-        for b in range(row_blocks):
-            @pl.when(sec == via[b])
-            def _():
-                first_hop(b).wait_recv()
-                second_hop(b).start()
-
     valid = sec > 0
     rebuilt_copies = []
 
@@ -205,9 +256,8 @@
             fill(b).wait()
 
         lists = meta_in[...]
-        lane = lax.broadcasted_iota(jnp.int32, (1, BLK), 1)
-        ids = jnp.where((lane < lists[1:2, :]) & valid, lists[0:1, :], -1)
-        listed = (lane < lists[4:5, :]) & (lists[2:3, :] == b) & valid
+        refreshed = jnp.where((lane < lists[1:2, :]) & valid, lists[0:1, :], -1)
+        listed = (lane < lists[4:5, :]) & (lane < ids.shape[1]) & (lists[2:3, :] == b) & valid
         factor = jnp.sum(jnp.where(listed, lists[3:4, :].astype(jnp.float32) / 4096.0, 0.0), axis=1, keepdims=True)
         strip = 16
 
@@ -215,7 +265,7 @@
             start = pl.multiple_of(b * BLK + i * strip, strip)
             rows = pl.ds(start, strip)
             number = lax.broadcasted_iota(jnp.int32, (strip, BLK), 0) + start
-            hit = jnp.max(jnp.where(number == ids, 1.0, 0.0), axis=1, keepdims=True) > 0.0
+            hit = jnp.max(jnp.where(number == refreshed, 1.0, 0.0), axis=1, keepdims=True) > 0.0
             came = pay[rows, :].astype(jnp.float32)
             delta = (came * factor).astype(jnp.bfloat16).astype(jnp.float32)
             mixed = jnp.where(hit, came, held[rows, :].astype(jnp.float32) + delta).astype(jnp.bfloat16)
@@ -231,8 +281,8 @@
         rebuilt_copies.append(copy)
 
     def out_copy(j):
-        cols = pl.ds(pl.multiple_of(j * COLS, COLS), COLS)
-        return pltpu.make_async_copy(outbuf.at[j], qkv_out.at[:, cols], out_sem.at[j])
+        out, k = (q_out, j) if j < q_blocks else (kv_out, j - q_blocks)
+        return pltpu.make_async_copy(outbuf.at[j], out.at[:, pl.ds(k * COLS, COLS)], out_sem.at[j])
 
     def compute(g):
         a = g * GRP
@@ -243,48 +293,51 @@
             total = jnp.dot(normed[...], wbuf[j], preferred_element_type=jnp.float32)
             cols = pl.ds(pl.multiple_of(j * COLS, COLS), COLS)
             outbuf[j] = (total + bias[:, cols]).astype(jnp.bfloat16)
+            return carry
+
+        lax.fori_loop(a, a + GRP, one, 0)
+        for j in range(a, a + GRP):
             out_copy(j).start()
-            return carry
-
-        lax.fori_loop(a, a + GRP, one, 0)
 
     level1(0)
     level1(1)
+    relay_step(0)
+    relay_step(3)
+    for g in range(groups // 2, groups):
+        own_x(g)
     load_cache.wait()
 
     @pl.when(sec != 0)
     def _():
         meta_copy().wait_recv()
 
-    @pl.when(sec == 0)
-    def _():
-        fill_meta.wait()
-
-    relay_step()
-    rebuild(0)
-    rebuild(1)
+    relay_step(1)
+    relay_step(2)
     level2(0)
     level1(2)
-    rebuild(2)
+    relay_end(3)
+    rebuild(0)
     level2(1)
     level3(0)
     level1(3)
+    rebuild(1)
     level2(2)
     level3(1)
     level1(4)
+    rebuild(2)
     rebuild(3)
+    compute(0)
     level2(3)
     level3(2)
     level1(5)
-    compute(0)
     compute(1)
+    compute(2)
     level2(4)
     level3(3)
-    compute(2)
     compute(3)
-    level2(5)
     level3(4)
     compute(4)
+    level2(5)
     level3(5)
     compute(5)
 
@@ -304,7 +357,11 @@
     for b in range(row_blocks):
         @pl.when(sec == via[b])
         def _():
-            second_hop(b).wait_send()
+            (last_hop(b) if via[b] else middle_hop()).wait_send()
+
+    @pl.when(sec == 0)
+    def _():
+        last_hop(3).wait_send()
 
 
 def body(
@@ -318,31 +375,18 @@
     groups = blocks // GRP
     row_blocks = rows // BLK
 
-    def lanes(v):
-        return jnp.pad(v.reshape(1, -1), ((0, 0), (0, BLK - v.size)))
-
-    meta = jnp.concatenate(
-        [
-            lanes(refresh_ids[0, 0]),
-            jnp.broadcast_to(refresh_counts[0, 0], (1, BLK)),
-            lanes(block_ids[0, 0]),
-            lanes(block_scales[0, 0]),
-            jnp.broadcast_to(block_counts[0, 0], (1, BLK)),
-            jnp.zeros((3, BLK), jnp.int32),
-        ],
-        axis=0,
-    )
     anywhere = pl.BlockSpec(memory_space=pl.ANY)
     vmem = pl.BlockSpec(memory_space=pltpu.VMEM)
     dma = pltpu.SemaphoreType.DMA
-    rebuilt, qkv = pl.pallas_call(
+    rebuilt, queries, keys_values = pl.pallas_call(
         kernel,
         out_shape=(
             jax.ShapeDtypeStruct((rows, feature), jnp.bfloat16),
-            jax.ShapeDtypeStruct((rows, q_cols + kv_cols), jnp.bfloat16),
+            jax.ShapeDtypeStruct((rows, q_cols), jnp.bfloat16),
+            jax.ShapeDtypeStruct((rows, kv_cols), jnp.bfloat16),
         ),
-        in_specs=[anywhere, anywhere, anywhere, vmem, anywhere, vmem, anywhere, vmem],
-        out_specs=(anywhere, anywhere),
+        in_specs=[anywhere, anywhere, vmem, vmem, vmem, vmem, vmem, vmem, anywhere, vmem, anywhere, vmem],
+        out_specs=(anywhere, anywhere, anywhere),
         scratch_shapes=[
             pltpu.VMEM((blocks, feature, COLS), jnp.bfloat16),
             pltpu.VMEM((rows, feature), jnp.bfloat16),
@@ -350,6 +394,8 @@
             pltpu.VMEM((rows, feature), jnp.bfloat16),
             pltpu.VMEM((blocks, rows, COLS), jnp.bfloat16),
             pltpu.VMEM((BLK, feature), jnp.bfloat16),
+            pltpu.VMEM((BLK, feature), jnp.bfloat16),
+            pltpu.VMEM((8, BLK), jnp.int32),
             pltpu.VMEM((8, BLK), jnp.int32),
             pltpu.VMEM((1, q_cols + kv_cols), jnp.float32),
             dma((blocks,)),
@@ -362,13 +408,18 @@
             dma,
             dma,
             dma,
+            dma,
+            dma,
             dma((row_blocks,)),
             dma((blocks,)),
         ],
-        compiler_params=pltpu.CompilerParams(has_side_effects=True, vmem_limit_bytes=64 * 1024 * 1024 - 65536),
+        compiler_params=pltpu.CompilerParams(collective_id=0, has_side_effects=True, vmem_limit_bytes=64 * 1024 * 1024 - 65536),
         name="boundary",
-    )(cache[0], payload[0], meta, norm_gain, query_weight[0], query_bias, kv_weight[0], kv_bias)
-    return rebuilt[None], qkv[None, :, :q_cols], qkv[None, :, q_cols:]
+    )(
+        cache[0], payload[0], block_ids[0], block_counts, block_scales[0], refresh_ids[0], refresh_counts,
+        norm_gain, query_weight[0], query_bias, kv_weight[0], kv_bias,
+    )
+    return rebuilt[None], queries[None], keys_values[None]
 
 
 def solution(mesh):

time: 188 us -> 148 us (0.79)
  the two profiles are of different devices: /device:TPU:6 before, /device:TPU:1 now
where the time goes in v2:
time: 148 us; the launch traced here: 146 us
  Pallas kernels  137 us (93%)
  local copies, waits for them, and re-layouts  7.19 us (5%)
  between operations  1.94 us (1%)
    pallas_call x1, Pallas kernels, body(): pl.pallas_call(kernel, out_shape=(jax.ShapeDtypeStruct((rows, feature), j...  137 us
    unnamed x7, local copies, waits for them, and re-layouts  7.19 us

profile of v2, /device:TPU:1, one launch (start us, length us, event | category | flops | bytes accessed | tf_op | source)
XLA Modules:
  0.0 145.8 jit_solution(11268301949816895929)
XLA Ops:
  1.9 136.7 %boundary.1 = (bf16[512,3584]{1,0:T(8,128)(2,1)}, bf16[512,3584]{1,0:T(8,128)(2,1)}, bf16[512,1024]{1,0:T(8,128)(2,1)}) custom-call(bf16[512,3584]{1,0:T(8,128)(2,1)} %bitcast.12, bf16[512,3584]{1,0:T(8,128)(2,1)} %bitcast.13, s32[1,2]{1,0:T(1,128)} %bitcast.17, s32[1,1]{1,0:T(1,128)S(6)} %copy.18.counts, s32[1,2]{1,0:T(1,128)} %bitcast.18, ...), custom_call_target="tpu_custom_call" | custom-call | tf_op jit(solution)/shard_map/boundary/pallas_call | solution.py:381
  138.6 0.0 copy-start
  138.6 4.3 %copy.20 = bf16[1,512,3584]{2,1,0:T(8,128)(2,1)} copy(bf16[1,512,3584]{2,1,0:T(8,128)(2,1)} %bitcast.11) | data formatting | bytes 7340032
  142.9 0.0 copy-done
  142.9 0.0 copy-start.1
  142.9 1.8 %copy.21 = bf16[1,512,3584]{2,1,0:T(8,128)(2,1)} copy(bf16[1,512,3584]{2,1,0:T(8,128)(2,1)S(1)} %bitcast.10) | data formatting | bytes 7340032
  144.7 0.1 copy-done.1
  144.9 1.0 copy.22
Async XLA Ops:
  138.6 4.3 %copy-start = (bf16[512,3584]{1,0:T(8,128)(2,1)S(1)}, bf16[512,3584]{1,0:T(8,128)(2,1)}, u32[]{:S(2)}) copy-start(bf16[512,3584]{1,0:T(8,128)(2,1)} %get-tuple-element.7) | copy-start | bytes 11010052
  142.9 2.0 %copy-start.1 = (bf16[512,1024]{1,0:T(8,128)(2,1)S(1)}, bf16[512,1024]{1,0:T(8,128)(2,1)}, u32[]{:S(2)}) copy-start(bf16[512,1024]{1,0:T(8,128)(2,1)} %get-tuple-element.8) | copy-start | bytes 3145732

commit v3 on v2

--- a/solution.py
+++ b/solution.py
@@ -18,15 +18,16 @@
 XYM_BC, XYP_BC, XYP_A, XYM_A = 7, 8, 9, 10
 XY2B, XY2C, XY2A = 11, 12, 13
 D_YM, D_YP, D_XP, D_Y2, D_XYM, D_XYP, D_XY2 = 14, 15, 16, 17, 18, 19, 20
-CLASSES = 21
+D_XYM_A, D_XYP_A, D_XY2_A = 21, 22, 23
+CLASSES = 24
 
 
 def kernel(
     cache, payload, ids, counts, scales, refresh_ids, refresh_counts, gain, q_w, q_b, kv_w, kv_b,
     rebuilt_out, q_out, kv_out,
-    wbuf, pay, held, normed, outbuf, relay, relay_two, meta, meta_in, bias,
+    wbuf, pay, held, normed, outbuf, partial, relay, relay_two, relay_three, meta, meta_in, bias,
     ld_sem, cache_sem, send, recv, pay_send, pay_recv, meta_send, meta_recv,
-    relay_send, relay_recv, two_send, two_recv, reb_sem, out_sem,
+    relay_send, relay_recv, two_send, two_recv, three_send, three_recv, reb_sem, out_sem,
 ):
     sec = lax.axis_index("section")
     me = lax.axis_index("rep")
@@ -54,7 +55,7 @@
 
     def remote(ref, cls, g, to):
         return pltpu.make_async_remote_copy(
-            src_ref=ref, dst_ref=ref, send_sem=send.at[cls, g], recv_sem=recv.at[cls, g],
+            src_ref=ref, dst_ref=ref, send_sem=send, recv_sem=recv.at[cls, g],
             device_id=(sec, to), device_id_type=MESH,
         )
 
@@ -63,7 +64,7 @@
     def push(r, first, count, cls, g, to):
         copy = remote(region(r, first, count), cls, g, to)
         copy.start()
-        sent.append(copy)
+        sent.append(count)
 
     def arrive(r, first, count, cls, g):
         remote(region(r, first, count), cls, g, other).wait_recv()
@@ -128,32 +129,57 @@
         )
 
     following = lax.rem(sec + 1, last + 1)
-    via = (half, half - 1, last, 0)
 
     def direct(b):
         return pay_copy(block(payload, b), block(pay, b), following, me, pay_send.at[b], pay_recv.at[b])
 
     def first_hop(b):
-        return pay_copy(block(payload, b), relay, via[b], xp if via[b] else me, pay_send.at[b], relay_recv)
-
-    def middle_hop():
-        return pay_copy(relay, relay_two, 0, xp, relay_send, two_recv)
+        to_sec, to_rep = ((last, xp), (half - 1, xp), (0, me), (0, me))[b]
+        dst, sem = (relay_two, two_recv) if b == 3 else (relay, relay_recv)
+        return pay_copy(block(payload, b), dst, to_sec, to_rep, pay_send.at[b], sem)
+
+    def over():
+        return pay_copy(relay, relay, half, xp, relay_send, relay_recv)
+
+    def across():
+        return pay_copy(relay_two, relay_three, 0, xp, two_send, three_recv)
 
     def last_hop(b):
-        src, sem = (relay, relay_send) if via[b] else (relay_two, two_send)
+        src, sem = (relay_three, three_send) if b == 3 else (relay, relay_send)
         return pay_copy(src, block(pay, b), half, xp, sem, pay_recv.at[b])
 
-    def relay_step(b):
-        @pl.when(sec == via[b])
-        def _():
-            first_hop(b).wait_recv()
-            (last_hop(b) if via[b] else middle_hop()).start()
-
-    def relay_end(b):
+    def relay_first():
+        @pl.when(sec == last)
+        def _():
+            first_hop(0).wait_recv()
+            last_hop(0).start()
+
         @pl.when(sec == 0)
         def _():
-            middle_hop().wait_recv()
-            last_hop(b).start()
+            first_hop(2).wait_recv()
+            over().start()
+
+    def relay_second():
+        @pl.when(sec == half - 1)
+        def _():
+            first_hop(1).wait_recv()
+            last_hop(1).start()
+
+        @pl.when(sec == half)
+        def _():
+            over().wait_recv()
+            last_hop(2).start()
+
+        @pl.when(sec == 0)
+        def _():
+            first_hop(3).wait_recv()
+            across().start()
+
+    def relay_third():
+        @pl.when(sec == 0)
+        def _():
+            across().wait_recv()
+            last_hop(3).start()
 
     def meta_copy():
         return pay_copy(meta, meta_in, following, me, meta_send, meta_recv)
@@ -203,22 +229,26 @@
 
     def level1(g):
         a = g * GRP
+        there, source = (yp, ym) if g % 2 == 0 else (ym, yp)
+        final = g == groups - 1
+        arrive(ym, a, GRP, YM, g)
+        arrive(yp, a, GRP, YP, g)
+        if final:
+            push(source, a, 1, Y2A, g, there)
         arrive(xp, a, GRP, XP, g)
         push(xp, a + 1, 2, XYM_BC, g, yp)
         push(xp, a + 1, 2, XYP_BC, g, ym)
+        push(ym, a + 1, 1, Y2B, g, yp)
+        push(yp, a + 2, 1, Y2C, g, ym)
+        if not final:
+            push(source, a, 1, Y2A, g, there)
         push(xp, a, GRP, D_XP, g, other)
-        arrive(ym, a, GRP, YM, g)
-        push(ym, a + 1, 1, Y2B, g, yp)
-        if g % 2 == 0:
-            push(ym, a, 1, Y2A, g, yp)
-        push(ym, a, 1, XYM_A, g, xp)
         push(ym, a, GRP, D_YM, g, other)
-        arrive(yp, a, GRP, YP, g)
-        push(yp, a + 2, 1, Y2C, g, ym)
-        if g % 2 == 1:
-            push(yp, a, 1, Y2A, g, ym)
-        push(yp, a, 1, XYP_A, g, xp)
         push(yp, a, GRP, D_YP, g, other)
+
+    def beside(g):
+        push(ym, g * GRP, 1, XYM_A, g, xp)
+        push(yp, g * GRP, 1, XYP_A, g, xp)
 
     def level2(g):
         a = g * GRP
@@ -226,22 +256,33 @@
         push(xym, a + 1, 1, XY2B, g, yp)
         arrive(xyp, a + 1, 2, XYP_BC, g)
         push(xyp, a + 2, 1, XY2C, g, ym)
-        arrive(y2, a, 1, Y2A, g)
-        push(y2, a, 1, XY2A, g, xp)
+        push(xym, a + 1, 2, D_XYM, g, other)
+        push(xyp, a + 1, 2, D_XYP, g, other)
+
+    def opposite_a(g):
+        arrive(y2, g * GRP, 1, Y2A, g)
+        push(y2, g * GRP, 1, XY2A, g, xp)
+
+    def opposite(g):
+        a = g * GRP
         arrive(y2, a + 1, 1, Y2B, g)
         arrive(y2, a + 2, 1, Y2C, g)
         push(y2, a, GRP, D_Y2, g, other)
-        arrive(xym, a, 1, XYM_A, g)
-        push(xym, a, GRP, D_XYM, g, other)
-        arrive(xyp, a, 1, XYP_A, g)
-        push(xyp, a, GRP, D_XYP, g, other)
-
-    def level3(g):
+
+    def far(g):
         a = g * GRP
         arrive(xy2, a + 1, 1, XY2B, g)
         arrive(xy2, a + 2, 1, XY2C, g)
+        push(xy2, a + 1, 2, D_XY2, g, other)
+
+    def sides(g):
+        a = g * GRP
+        arrive(xym, a, 1, XYM_A, g)
+        push(xym, a, 1, D_XYM_A, g, other)
+        arrive(xyp, a, 1, XYP_A, g)
+        push(xyp, a, 1, D_XYP_A, g, other)
         arrive(xy2, a, 1, XY2A, g)
-        push(xy2, a, GRP, D_XY2, g, other)
+        push(xy2, a, 1, D_XY2_A, g, other)
 
     valid = sec > 0
     rebuilt_copies = []
@@ -284,65 +325,148 @@
         out, k = (q_out, j) if j < q_blocks else (kv_out, j - q_blocks)
         return pltpu.make_async_copy(outbuf.at[j], out.at[:, pl.ds(k * COLS, COLS)], out_sem.at[j])
 
-    def compute(g):
+    def product(j, start, size):
+        part = pl.ds(pl.multiple_of(start, BLK), size)
+        return jnp.dot(normed[:, part], wbuf[j, part, :], preferred_element_type=jnp.float32)
+
+    def finish(j, total):
+        cols = pl.ds(pl.multiple_of(j * COLS, COLS), COLS)
+        outbuf[j] = (total + bias[:, cols]).astype(jnp.bfloat16)
+
+    def near(g):
+        for r, cls in ((me, SIB), (ym, D_YM), (yp, D_YP), (xp, D_XP), (y2, D_Y2)):
+            arrive(twin(r), g * GRP, GRP, cls, g)
+        for r, cls in ((xym, D_XYM), (xyp, D_XYP)):
+            arrive(twin(r), g * GRP + 1, 2, cls, g)
+
+    def pair(g):
+        near(g)
+        arrive(twin(xy2), g * GRP + 1, 2, D_XY2, g)
+
+        def one(j, carry):
+            finish(j, product(j, 0, normed.shape[1]))
+            return carry
+
+        lax.fori_loop(g * GRP + 1, (g + 1) * GRP, one, 0)
+        for j in range(g * GRP + 1, (g + 1) * GRP):
+            out_copy(j).start()
+
+    def single(g):
         a = g * GRP
-        for r, cls in ((me, SIB), (ym, D_YM), (yp, D_YP), (xp, D_XP), (y2, D_Y2), (xym, D_XYM), (xyp, D_XYP), (xy2, D_XY2)):
-            arrive(twin(r), a, GRP, cls, g)
+        for r, cls in ((xym, D_XYM_A), (xyp, D_XYP_A), (xy2, D_XY2_A)):
+            arrive(twin(r), a, 1, cls, g)
 
         def one(j, carry):
-            total = jnp.dot(normed[...], wbuf[j], preferred_element_type=jnp.float32)
-            cols = pl.ds(pl.multiple_of(j * COLS, COLS), COLS)
-            outbuf[j] = (total + bias[:, cols]).astype(jnp.bfloat16)
+            finish(j, product(j, 0, normed.shape[1]))
             return carry
 
-        lax.fori_loop(a, a + GRP, one, 0)
-        for j in range(a, a + GRP):
+        lax.fori_loop(a, a + 1, one, 0)
+        out_copy(a).start()
+
+    side = normed.shape[1] // 2
+    mine, yours = x * side, (1 - x) * side
+    late = (((y + 2) % 4) // 2) * (side // 2)
+
+    def prepare(g):
+        near(g)
+
+        def one(k, carry):
+            partial[k] = product(g * GRP + 1 + k, mine, side) + product(g * GRP + 1 + k, yours + side // 2 - late, side // 2)
+            return carry
+
+        lax.fori_loop(0, GRP - 1, one, 0)
+
+    def complete(g):
+        a = g * GRP + 1
+        arrive(twin(xy2), a, 2, D_XY2, g)
+
+        def one(k, carry):
+            finish(a + k, partial[k] + product(a + k, yours + late, side // 2))
+            return carry
+
+        lax.fori_loop(0, GRP - 1, one, 0)
+        for j in range(a, a + GRP - 1):
             out_copy(j).start()
 
     level1(0)
     level1(1)
-    relay_step(0)
-    relay_step(3)
-    for g in range(groups // 2, groups):
-        own_x(g)
+    relay_first()
+    own_x(3)
+    beside(0)
+    beside(1)
+    relay_second()
+    own_x(4)
     load_cache.wait()
 
     @pl.when(sec != 0)
     def _():
         meta_copy().wait_recv()
 
-    relay_step(1)
-    relay_step(2)
     level2(0)
     level1(2)
-    relay_end(3)
+    beside(2)
+    opposite_a(0)
+    opposite(0)
+    own_x(5)
     rebuild(0)
+    relay_third()
     level2(1)
-    level3(0)
     level1(3)
+    beside(3)
+    opposite_a(1)
+    opposite(1)
+    far(0)
     rebuild(1)
     level2(2)
-    level3(1)
     level1(4)
+    beside(4)
+    opposite_a(2)
+    opposite(2)
+    far(1)
     rebuild(2)
     rebuild(3)
-    compute(0)
+    pair(0)
     level2(3)
-    level3(2)
+    opposite_a(3)
+    opposite(3)
+    sides(0)
+    pair(1)
+    far(2)
+    single(0)
+    level2(4)
     level1(5)
-    compute(1)
-    compute(2)
-    level2(4)
-    level3(3)
-    compute(3)
-    level3(4)
-    compute(4)
+    beside(5)
+    pair(2)
+    sides(1)
+    opposite_a(4)
+    opposite(4)
+    single(1)
+    far(3)
+    sides(2)
+    far(4)
+    pair(3)
+    opposite_a(5)
+    single(2)
+    pair(4)
     level2(5)
-    level3(5)
-    compute(5)
-
-    for copy in sent:
-        copy.wait_send()
+    sides(3)
+    sides(4)
+    opposite(5)
+    single(3)
+    single(4)
+    sides(5)
+    far(5)
+    prepare(5)
+    single(5)
+    complete(5)
+
+    slabs, left = divmod(sum(sent), blocks)
+    assert left == 0
+    everything = wbuf.at[:, pl.ds(0, slabs * depth), :]
+    pltpu.make_async_remote_copy(
+        src_ref=everything, dst_ref=everything, send_sem=send, recv_sem=recv.at[0, 0],
+        device_id=(sec, other), device_id_type=MESH,
+    ).wait_send()
     for copy in rebuilt_copies:
         copy.wait()
     for j in range(blocks):
@@ -354,13 +478,22 @@
         for b in range(row_blocks):
             direct(b).wait_send()
 
-    for b in range(row_blocks):
-        @pl.when(sec == via[b])
-        def _():
-            (last_hop(b) if via[b] else middle_hop()).wait_send()
+    @pl.when(sec == last)
+    def _():
+        last_hop(0).wait_send()
+
+    @pl.when(sec == half - 1)
+    def _():
+        last_hop(1).wait_send()
+
+    @pl.when(sec == half)
+    def _():
+        last_hop(2).wait_send()
 
     @pl.when(sec == 0)
     def _():
+        over().wait_send()
+        across().wait_send()
         last_hop(3).wait_send()
 
 
@@ -393,6 +526,8 @@
             pltpu.VMEM((rows, feature), jnp.bfloat16),
             pltpu.VMEM((rows, feature), jnp.bfloat16),
             pltpu.VMEM((blocks, rows, COLS), jnp.bfloat16),
+            pltpu.VMEM((GRP - 1, rows, COLS), jnp.float32),
+            pltpu.VMEM((BLK, feature), jnp.bfloat16),
             pltpu.VMEM((BLK, feature), jnp.bfloat16),
             pltpu.VMEM((BLK, feature), jnp.bfloat16),
             pltpu.VMEM((8, BLK), jnp.int32),
@@ -400,10 +535,12 @@
             pltpu.VMEM((1, q_cols + kv_cols), jnp.float32),
             dma((blocks,)),
             dma,
-            dma((CLASSES, groups)),
+            dma,
             dma((CLASSES, groups)),
             dma((row_blocks,)),
             dma((row_blocks,)),
+            dma,
+            dma,
             dma,
             dma,
             dma,

time: 148 us -> 139 us (0.939); the launches traced: 146 us -> 139 us
  Pallas kernels: 137 us -> 130 us
    pallas_call x1, Pallas kernels: 137 us -> 130 us  [body(): pl.pallas_call(kernel, out_shape=(jax.ShapeDtypeStruct((rows, feature), j...]
where the time goes in v3:
time: 139 us
  Pallas kernels  130 us (94%)
  local copies, waits for them, and re-layouts  7.19 us (5%)
  between operations  1.94 us (1%)
    pallas_call x1, Pallas kernels, body(): pl.pallas_call(kernel, out_shape=(jax.ShapeDtypeStruct((rows, feature), j...  130 us
    unnamed x7, local copies, waits for them, and re-layouts  7.19 us

profile of v3, /device:TPU:1, one launch (start us, length us, event | category | flops | bytes accessed | tf_op | source)
XLA Modules:
  0.0 139.0 jit_solution(17219685547437126289)
XLA Ops:
  1.9 129.9 %boundary.1 = (bf16[512,3584]{1,0:T(8,128)(2,1)}, bf16[512,3584]{1,0:T(8,128)(2,1)}, bf16[512,1024]{1,0:T(8,128)(2,1)}) custom-call(bf16[512,3584]{1,0:T(8,128)(2,1)} %bitcast.12, bf16[512,3584]{1,0:T(8,128)(2,1)} %bitcast.13, s32[1,2]{1,0:T(1,128)} %bitcast.17, s32[1,1]{1,0:T(1,128)S(6)} %copy.18.counts, s32[1,2]{1,0:T(1,128)} %bitcast.18, ...), custom_call_target="tpu_custom_call" | custom-call | tf_op jit(solution)/shard_map/boundary/pallas_call | solution.py:514
  131.8 0.0 copy-start
  131.8 4.3 %copy.20 = bf16[1,512,3584]{2,1,0:T(8,128)(2,1)} copy(bf16[1,512,3584]{2,1,0:T(8,128)(2,1)} %bitcast.11) | data formatting | bytes 7340032
  136.1 0.0 copy-done
  136.1 0.0 copy-start.1
  136.1 1.8 %copy.21 = bf16[1,512,3584]{2,1,0:T(8,128)(2,1)} copy(bf16[1,512,3584]{2,1,0:T(8,128)(2,1)S(1)} %bitcast.10) | data formatting | bytes 7340032
  137.9 0.1 copy-done.1
  138.1 1.0 copy.22
Async XLA Ops:
  131.8 4.3 %copy-start = (bf16[512,3584]{1,0:T(8,128)(2,1)S(1)}, bf16[512,3584]{1,0:T(8,128)(2,1)}, u32[]{:S(2)}) copy-start(bf16[512,3584]{1,0:T(8,128)(2,1)} %get-tuple-element.7) | copy-start | bytes 11010052
  136.1 2.0 %copy-start.1 = (bf16[512,1024]{1,0:T(8,128)(2,1)S(1)}, bf16[512,1024]{1,0:T(8,128)(2,1)}, u32[]{:S(2)}) copy-start(bf16[512,1024]{1,0:T(8,128)(2,1)} %get-tuple-element.8) | copy-start | bytes 3145732

commit v4 on v3

--- a/solution.py
+++ b/solution.py
@@ -13,21 +13,20 @@
 GRP = 3
 MESH = pl.DeviceIdType.MESH
 
-YM, YP, XP, SIB = 0, 1, 2, 3
-Y2B, Y2C, Y2A = 4, 5, 6
-XYM_BC, XYP_BC, XYP_A, XYM_A = 7, 8, 9, 10
-XY2B, XY2C, XY2A = 11, 12, 13
-D_YM, D_YP, D_XP, D_Y2, D_XYM, D_XYP, D_XY2 = 14, 15, 16, 17, 18, 19, 20
-D_XYM_A, D_XYP_A, D_XY2_A = 21, 22, 23
-CLASSES = 24
+YM, YP, XP = 0, 1, 2
+Y2B, Y2C, Y2A = 3, 4, 5
+XYM_BC, XYP_BC, XYP_A, XYM_A = 6, 7, 8, 9
+XY2B, XY2C, XY2A = 10, 11, 12
+D_OWN, D_SIDE, D_FAR, D_A = 13, 14, 15, 16
+CLASSES = 17
 
 
 def kernel(
     cache, payload, ids, counts, scales, refresh_ids, refresh_counts, gain, q_w, q_b, kv_w, kv_b,
-    rebuilt_out, q_out, kv_out,
-    wbuf, pay, held, normed, outbuf, partial, relay, relay_two, relay_three, meta, meta_in, bias,
+    held, outbuf,
+    wbuf, pay, normed, partial, relay, relay_two, relay_three, meta, meta_in, bias,
     ld_sem, cache_sem, send, recv, pay_send, pay_recv, meta_send, meta_recv,
-    relay_send, relay_recv, two_send, two_recv, three_send, three_recv, reb_sem, out_sem,
+    relay_send, relay_recv, two_send, two_recv, three_send, three_recv,
 ):
     sec = lax.axis_index("section")
     me = lax.axis_index("rep")
@@ -45,9 +44,6 @@
     ym, yp, y2 = rank(0, 3), rank(0, 1), rank(0, 2)
     xp, xym, xyp, xy2 = rank(1, 0), rank(1, 3), rank(1, 1), rank(1, 2)
     other = me + 1 - 2 * core
-
-    def twin(r):
-        return r + 1 - 2 * core
 
     def region(r, first, count):
         rows = pl.ds(pl.multiple_of(r * depth, 32), depth)
@@ -222,7 +218,7 @@
             def _():
                 first_hop(1).start()
 
-        push(me, g * GRP, GRP, SIB, g, other)
+        push(me, g * GRP, GRP, D_OWN, g, other)
 
     bias[:, : q_w.shape[1]] = q_b[...]
     bias[:, q_w.shape[1] :] = kv_b[...]
@@ -242,9 +238,9 @@
         push(yp, a + 2, 1, Y2C, g, ym)
         if not final:
             push(source, a, 1, Y2A, g, there)
-        push(xp, a, GRP, D_XP, g, other)
-        push(ym, a, GRP, D_YM, g, other)
-        push(yp, a, GRP, D_YP, g, other)
+        push(xp, a, GRP, D_OWN, g, other)
+        push(ym, a, GRP, D_OWN, g, other)
+        push(yp, a, GRP, D_OWN, g, other)
 
     def beside(g):
         push(ym, g * GRP, 1, XYM_A, g, xp)
@@ -256,8 +252,8 @@
         push(xym, a + 1, 1, XY2B, g, yp)
         arrive(xyp, a + 1, 2, XYP_BC, g)
         push(xyp, a + 2, 1, XY2C, g, ym)
-        push(xym, a + 1, 2, D_XYM, g, other)
-        push(xyp, a + 1, 2, D_XYP, g, other)
+        push(xym, a + 1, 2, D_SIDE, g, other)
+        push(xyp, a + 1, 2, D_SIDE, g, other)
 
     def opposite_a(g):
         arrive(y2, g * GRP, 1, Y2A, g)
@@ -267,25 +263,24 @@
         a = g * GRP
         arrive(y2, a + 1, 1, Y2B, g)
         arrive(y2, a + 2, 1, Y2C, g)
-        push(y2, a, GRP, D_Y2, g, other)
+        push(y2, a, GRP, D_OWN, g, other)
 
     def far(g):
         a = g * GRP
         arrive(xy2, a + 1, 1, XY2B, g)
         arrive(xy2, a + 2, 1, XY2C, g)
-        push(xy2, a + 1, 2, D_XY2, g, other)
+        push(xy2, a + 1, 2, D_FAR, g, other)
 
     def sides(g):
         a = g * GRP
         arrive(xym, a, 1, XYM_A, g)
-        push(xym, a, 1, D_XYM_A, g, other)
+        push(xym, a, 1, D_A, g, other)
         arrive(xyp, a, 1, XYP_A, g)
-        push(xyp, a, 1, D_XYP_A, g, other)
+        push(xyp, a, 1, D_A, g, other)
         arrive(xy2, a, 1, XY2A, g)
-        push(xy2, a, 1, D_XY2_A, g, other)
+        push(xy2, a, 1, D_A, g, other)
 
     valid = sec > 0
-    rebuilt_copies = []
 
     def rebuild(b):
         @pl.when(sec != 0)
@@ -317,13 +312,8 @@
             return carry
 
         lax.fori_loop(0, BLK // strip, one, 0)
-        copy = pltpu.make_async_copy(block(held, b), block(rebuilt_out, b), reb_sem.at[b])
-        copy.start()
-        rebuilt_copies.append(copy)
-
-    def out_copy(j):
-        out, k = (q_out, j) if j < q_blocks else (kv_out, j - q_blocks)
-        return pltpu.make_async_copy(outbuf.at[j], out.at[:, pl.ds(k * COLS, COLS)], out_sem.at[j])
+
+    once = jnp.where(me >= 0, 1, 0)
 
     def product(j, start, size):
         part = pl.ds(pl.multiple_of(start, BLK), size)
@@ -333,35 +323,33 @@
         cols = pl.ds(pl.multiple_of(j * COLS, COLS), COLS)
         outbuf[j] = (total + bias[:, cols]).astype(jnp.bfloat16)
 
+    def handed(first, count, shards, cls, g):
+        whole = wbuf.at[pl.ds(first, count), pl.ds(0, shards * depth), :]
+        remote(whole, cls, g, other).wait_recv()
+
     def near(g):
-        for r, cls in ((me, SIB), (ym, D_YM), (yp, D_YP), (xp, D_XP), (y2, D_Y2)):
-            arrive(twin(r), g * GRP, GRP, cls, g)
-        for r, cls in ((xym, D_XYM), (xyp, D_XYP)):
-            arrive(twin(r), g * GRP + 1, 2, cls, g)
+        handed(g * GRP, GRP, 5, D_OWN, g)
+        handed(g * GRP + 1, 2, 2, D_SIDE, g)
 
     def pair(g):
         near(g)
-        arrive(twin(xy2), g * GRP + 1, 2, D_XY2, g)
+        handed(g * GRP + 1, 2, 1, D_FAR, g)
 
         def one(j, carry):
             finish(j, product(j, 0, normed.shape[1]))
             return carry
 
         lax.fori_loop(g * GRP + 1, (g + 1) * GRP, one, 0)
-        for j in range(g * GRP + 1, (g + 1) * GRP):
-            out_copy(j).start()
 
     def single(g):
         a = g * GRP
-        for r, cls in ((xym, D_XYM_A), (xyp, D_XYP_A), (xy2, D_XY2_A)):
-            arrive(twin(r), a, 1, cls, g)
+        handed(a, 1, 3, D_A, g)
 
         def one(j, carry):
             finish(j, product(j, 0, normed.shape[1]))
             return carry
 
-        lax.fori_loop(a, a + 1, one, 0)
-        out_copy(a).start()
+        lax.fori_loop(a, a + once, one, 0)
 
     side = normed.shape[1] // 2
     mine, yours = x * side, (1 - x) * side
@@ -378,15 +366,13 @@
 
     def complete(g):
         a = g * GRP + 1
-        arrive(twin(xy2), a, 2, D_XY2, g)
+        handed(a, 2, 1, D_FAR, g)
 
         def one(k, carry):
             finish(a + k, partial[k] + product(a + k, yours + late, side // 2))
             return carry
 
         lax.fori_loop(0, GRP - 1, one, 0)
-        for j in range(a, a + GRP - 1):
-            out_copy(j).start()
 
     level1(0)
     level1(1)
@@ -433,32 +419,32 @@
     pair(1)
     far(2)
     single(0)
+    pair(2)
+    sides(1)
     level2(4)
     level1(5)
     beside(5)
-    pair(2)
-    sides(1)
+    single(1)
+    sides(2)
     opposite_a(4)
     opposite(4)
-    single(1)
+    single(2)
     far(3)
-    sides(2)
+    sides(3)
     far(4)
     pair(3)
     opposite_a(5)
-    single(2)
+    single(3)
     pair(4)
     level2(5)
-    sides(3)
     sides(4)
     opposite(5)
-    single(3)
     single(4)
+    prepare(5)
+    far(5)
     sides(5)
-    far(5)
-    prepare(5)
+    complete(5)
     single(5)
-    complete(5)
 
     slabs, left = divmod(sum(sent), blocks)
     assert left == 0
@@ -467,11 +453,6 @@
         src_ref=everything, dst_ref=everything, send_sem=send, recv_sem=recv.at[0, 0],
         device_id=(sec, other), device_id_type=MESH,
     ).wait_send()
-    for copy in rebuilt_copies:
-        copy.wait()
-    for j in range(blocks):
-        out_copy(j).wait()
-
     @pl.when(sec != last)
     def _():
         meta_copy().wait_send()
@@ -495,6 +476,18 @@
         over().wait_send()
         across().wait_send()
         last_hop(3).wait_send()
+
+
+def write(held, outbuf, rebuilt, queries, keys_values, sem):
+    q_blocks = queries.shape[1] // COLS
+    copies = [pltpu.make_async_copy(held, rebuilt, sem.at[outbuf.shape[0]])]
+    for j in range(outbuf.shape[0]):
+        out, k = (queries, j) if j < q_blocks else (keys_values, j - q_blocks)
+        copies.append(pltpu.make_async_copy(outbuf.at[j], out.at[:, pl.ds(k * COLS, COLS)], sem.at[j]))
+    for copy in copies:
+        copy.start()
+    for copy in copies:
+        copy.wait()
 
 
 def body(
@@ -511,21 +504,18 @@
     anywhere = pl.BlockSpec(memory_space=pl.ANY)
     vmem = pl.BlockSpec(memory_space=pltpu.VMEM)
     dma = pltpu.SemaphoreType.DMA
-    rebuilt, queries, keys_values = pl.pallas_call(
+    held, outbuf = pl.pallas_call(
         kernel,
         out_shape=(
-            jax.ShapeDtypeStruct((rows, feature), jnp.bfloat16),
-            jax.ShapeDtypeStruct((rows, q_cols), jnp.bfloat16),
-            jax.ShapeDtypeStruct((rows, kv_cols), jnp.bfloat16),
+            pltpu.VMEM((rows, feature), jnp.bfloat16),
+            pltpu.VMEM((blocks, rows, COLS), jnp.bfloat16),
         ),
         in_specs=[anywhere, anywhere, vmem, vmem, vmem, vmem, vmem, vmem, anywhere, vmem, anywhere, vmem],
-        out_specs=(anywhere, anywhere, anywhere),
+        out_specs=(vmem, vmem),
         scratch_shapes=[
             pltpu.VMEM((blocks, feature, COLS), jnp.bfloat16),
             pltpu.VMEM((rows, feature), jnp.bfloat16),
             pltpu.VMEM((rows, feature), jnp.bfloat16),
-            pltpu.VMEM((rows, feature), jnp.bfloat16),
-            pltpu.VMEM((blocks, rows, COLS), jnp.bfloat16),
             pltpu.VMEM((GRP - 1, rows, COLS), jnp.float32),
             pltpu.VMEM((BLK, feature), jnp.bfloat16),
             pltpu.VMEM((BLK, feature), jnp.bfloat16),
@@ -547,15 +537,22 @@
             dma,
             dma,
             dma,
-            dma((row_blocks,)),
-            dma((blocks,)),
         ],
-        compiler_params=pltpu.CompilerParams(collective_id=0, has_side_effects=True, vmem_limit_bytes=64 * 1024 * 1024 - 65536),
+        compiler_params=pltpu.CompilerParams(collective_id=0, has_side_effects=True, vmem_limit_bytes=48 * 1024 * 1024),
         name="boundary",
     )(
         cache[0], payload[0], block_ids[0], block_counts, block_scales[0], refresh_ids[0], refresh_counts,
         norm_gain, query_weight[0], query_bias, kv_weight[0], kv_bias,
     )
+    rebuilt, queries, keys_values = pl.pallas_call(
+        write,
+        out_shape=tuple(jax.ShapeDtypeStruct((rows, n), jnp.bfloat16) for n in (feature, q_cols, kv_cols)),
+        in_specs=[vmem, vmem],
+        out_specs=(anywhere, anywhere, anywhere),
+        scratch_shapes=[dma((blocks + 1,))],
+        compiler_params=pltpu.CompilerParams(vmem_limit_bytes=1024 * 1024),
+        name="write",
+    )(held, outbuf)
     return rebuilt[None], queries[None], keys_values[None]
 
 

time: 139 us -> 133 us (0.957)
  local copies, waits for them, and re-layouts: 7.19 us -> 0 us
    unnamed x7 -> x0, local copies, waits for them, and re-layouts: 7.19 us -> none
    pallas_call x1 -> x2, Pallas kernels: 130 us -> 130 us  [the longest x1 127 us: body(): pl.pallas_call(kernel, out_shape=(pltpu.VMEM((rows, feature), jnp.bfloat1...]
where the time goes in v4:
time: 133 us; the launch traced here: 132 us
  Pallas kernels  130 us (98%)
  between operations  1.93 us (1%)
    pallas_call x1, Pallas kernels, body(): pl.pallas_call(kernel, out_shape=(pltpu.VMEM((rows, feature), jnp.bfloat1...  127 us
    pallas_call x1, Pallas kernels, body(): pl.pallas_call(write, out_shape=tuple((jax.ShapeDtypeStruct((rows, n), jn...  3.43 us

profile of v4, /device:TPU:1, one launch (start us, length us, event | category | flops | bytes accessed | tf_op | source)
XLA Modules:
  0.0 131.9 jit_solution(3662062855935416661)
XLA Ops:
  1.9 126.5 %boundary.1 = (bf16[512,3584]{1,0:T(8,128)(2,1)S(1)}, bf16[18,512,256]{2,1,0:T(8,128)(2,1)S(1)}) custom-call(bf16[512,3584]{1,0:T(8,128)(2,1)} %bitcast.10, bf16[512,3584]{1,0:T(8,128)(2,1)} %bitcast.11, s32[1,2]{1,0:T(1,128)} %bitcast.14, s32[1,1]{1,0:T(1,128)S(6)} %copy.15.counts, s32[1,2]{1,0:T(1,128)} %bitcast.15, s32[1,128]{1,0:T(1,128)} %bitcast.16, ...), custom_call_target="tpu_custom_call" | custom-call | tf_op jit(solution)/shard_map/boundary/pallas_call | solution.py:507
  128.5 3.4 %write.1 = (bf16[512,3584]{1,0:T(8,128)(2,1)}, bf16[512,3584]{1,0:T(8,128)(2,1)}, bf16[512,1024]{1,0:T(8,128)(2,1)}) custom-call(bf16[512,3584]{1,0:T(8,128)(2,1)S(1)} %get-tuple-element.8.held, bf16[18,512,256]{2,1,0:T(8,128)(2,1)S(1)} %get-tuple-element.9.outbuf), custom_call_target="tpu_custom_call" | custom-call | tf_op jit(solution)/shard_map/write/pallas_call | solution.py:547

commit v5 on v4

--- a/solution.py
+++ b/solution.py
@@ -17,8 +17,8 @@
 Y2B, Y2C, Y2A = 3, 4, 5
 XYM_BC, XYP_BC, XYP_A, XYM_A = 6, 7, 8, 9
 XY2B, XY2C, XY2A = 10, 11, 12
-D_OWN, D_SIDE, D_FAR, D_A = 13, 14, 15, 16
-CLASSES = 17
+D_OWN, D_SIDE, D_FAR, D_A, D_Y2 = 13, 14, 15, 16, 17
+CLASSES = 18
 
 
 def kernel(
@@ -101,18 +101,14 @@
     for r in (ym, yp, xp, other):
         greet(sec, r)
     expected = 4
-    pairs = [(s, s + 1, me) for s in range(last)]
-    pairs += [(0, half - 1, me), (half - 1, last, xp), (half - 1, half, xp), (half, last, xp), (0, half, xp)]
-    for one, two, r in pairs:
-        @pl.when(sec == one)
-        def _():
-            greet(two, r)
-
-        @pl.when(sec == two)
-        def _():
-            greet(one, r)
-
-        expected = expected + jnp.where((sec == one) | (sec == two), 1, 0)
+    links = [(s + 1, s, me) for s in range(last)]
+    links += [(0, half - 1, me), (last, half - 1, xp), (half, half - 1, xp), (half, last, xp), (half, 0, xp)]
+    for receiver, sender, r in links:
+        @pl.when(sec == receiver)
+        def _():
+            greet(sender, r)
+
+        expected = expected + jnp.where(sec == sender, 1, 0)
     pl.semaphore_wait(barrier, expected)
 
     def block(ref, b):
@@ -246,14 +242,19 @@
         push(ym, g * GRP, 1, XYM_A, g, xp)
         push(yp, g * GRP, 1, XYP_A, g, xp)
 
+    def level2_up(g):
+        arrive(xym, g * GRP + 1, 2, XYM_BC, g)
+        push(xym, g * GRP + 1, 1, XY2B, g, yp)
+        push(xym, g * GRP + 1, 2, D_SIDE, g, other)
+
+    def level2_down(g):
+        arrive(xyp, g * GRP + 1, 2, XYP_BC, g)
+        push(xyp, g * GRP + 2, 1, XY2C, g, ym)
+        push(xyp, g * GRP + 1, 2, D_SIDE, g, other)
+
     def level2(g):
-        a = g * GRP
-        arrive(xym, a + 1, 2, XYM_BC, g)
-        push(xym, a + 1, 1, XY2B, g, yp)
-        arrive(xyp, a + 1, 2, XYP_BC, g)
-        push(xyp, a + 2, 1, XY2C, g, ym)
-        push(xym, a + 1, 2, D_SIDE, g, other)
-        push(xyp, a + 1, 2, D_SIDE, g, other)
+        level2_up(g)
+        level2_down(g)
 
     def opposite_a(g):
         arrive(y2, g * GRP, 1, Y2A, g)
@@ -263,7 +264,7 @@
         a = g * GRP
         arrive(y2, a + 1, 1, Y2B, g)
         arrive(y2, a + 2, 1, Y2C, g)
-        push(y2, a, GRP, D_OWN, g, other)
+        push(y2, a, GRP, D_Y2, g, other)
 
     def far(g):
         a = g * GRP
@@ -328,11 +329,12 @@
         remote(whole, cls, g, other).wait_recv()
 
     def near(g):
-        handed(g * GRP, GRP, 5, D_OWN, g)
+        handed(g * GRP, GRP, 4, D_OWN, g)
         handed(g * GRP + 1, 2, 2, D_SIDE, g)
 
     def pair(g):
         near(g)
+        handed(g * GRP, GRP, 1, D_Y2, g)
         handed(g * GRP + 1, 2, 1, D_FAR, g)
 
         def one(j, carry):
@@ -352,14 +354,27 @@
         lax.fori_loop(a, a + once, one, 0)
 
     side = normed.shape[1] // 2
+    quarter = side // 2
     mine, yours = x * side, (1 - x) * side
-    late = (((y + 2) % 4) // 2) * (side // 2)
+    late = (((y + 2) % 4) // 2) * quarter
+    soon = quarter - late
 
     def prepare(g):
+        a = g * GRP + 1
         near(g)
 
         def one(k, carry):
-            partial[k] = product(g * GRP + 1 + k, mine, side) + product(g * GRP + 1 + k, yours + side // 2 - late, side // 2)
+            partial[k] = product(a + k, mine + soon, quarter) + product(a + k, yours + soon, quarter)
+            return carry
+
+        lax.fori_loop(0, GRP - 1, one, 0)
+
+    def extend(g):
+        a = g * GRP + 1
+        handed(g * GRP, GRP, 1, D_Y2, g)
+
+        def one(k, carry):
+            partial[k] += product(a + k, mine + late, quarter)
             return carry
 
         lax.fori_loop(0, GRP - 1, one, 0)
@@ -369,7 +384,7 @@
         handed(a, 2, 1, D_FAR, g)
 
         def one(k, carry):
-            finish(a + k, partial[k] + product(a + k, yours + late, side // 2))
+            finish(a + k, partial[k] + product(a + k, yours + late, quarter))
             return carry
 
         lax.fori_loop(0, GRP - 1, one, 0)
@@ -425,25 +440,27 @@
     level1(5)
     beside(5)
     single(1)
-    sides(2)
     opposite_a(4)
     opposite(4)
-    single(2)
     far(3)
-    sides(3)
     far(4)
+    sides(2)
     pair(3)
     opposite_a(5)
+    sides(3)
+    single(2)
+    pair(4)
+    level2_up(5)
+    level2_down(5)
+    opposite(5)
     single(3)
-    pair(4)
-    level2(5)
-    sides(4)
-    opposite(5)
-    single(4)
     prepare(5)
     far(5)
+    sides(4)
     sides(5)
+    extend(5)
     complete(5)
+    single(4)
     single(5)
 
     slabs, left = divmod(sum(sent), blocks)

time: 133 us -> 131 us (0.985)
  no operation moved by 1% of the time
where the time goes in v5:
time: 131 us
  Pallas kernels  129 us (98%)
  between operations  1.93 us (1%)
    pallas_call x1, Pallas kernels, body(): pl.pallas_call(kernel, out_shape=(pltpu.VMEM((rows, feature), jnp.bfloat1...  125 us
    pallas_call x1, Pallas kernels, body(): pl.pallas_call(write, out_shape=tuple((jax.ShapeDtypeStruct((rows, n), jn...  3.43 us

profile of v5, /device:TPU:1, one launch (start us, length us, event | category | flops | bytes accessed | tf_op | source)
XLA Modules:
  0.0 130.7 jit_solution(1582572887835039651)
XLA Ops:
  1.9 125.4 %boundary.1 = (bf16[512,3584]{1,0:T(8,128)(2,1)S(1)}, bf16[18,512,256]{2,1,0:T(8,128)(2,1)S(1)}) custom-call(bf16[512,3584]{1,0:T(8,128)(2,1)} %bitcast.10, bf16[512,3584]{1,0:T(8,128)(2,1)} %bitcast.11, s32[1,2]{1,0:T(1,128)} %bitcast.14, s32[1,1]{1,0:T(1,128)S(6)} %copy.15.counts, s32[1,2]{1,0:T(1,128)} %bitcast.15, s32[1,128]{1,0:T(1,128)} %bitcast.16, ...), custom_call_target="tpu_custom_call" | custom-call | tf_op jit(solution)/shard_map/boundary/pallas_call | solution.py:524
  127.3 3.4 %write.1 = (bf16[512,3584]{1,0:T(8,128)(2,1)}, bf16[512,3584]{1,0:T(8,128)(2,1)}, bf16[512,1024]{1,0:T(8,128)(2,1)}) custom-call(bf16[512,3584]{1,0:T(8,128)(2,1)S(1)} %get-tuple-element.8.held, bf16[18,512,256]{2,1,0:T(8,128)(2,1)S(1)} %get-tuple-element.9.outbuf), custom_call_target="tpu_custom_call" | custom-call | tf_op jit(solution)/shard_map/write/pallas_call | solution.py:564

commit v6 on v5

--- a/solution.py
+++ b/solution.py
@@ -21,10 +21,15 @@
 CLASSES = 18
 
 
+def quarters(x, y, extent):
+    side = extent // 2
+    return side, side // 2, (((y + 2) % 4) // 2) * (side // 2)
+
+
 def kernel(
     cache, payload, ids, counts, scales, refresh_ids, refresh_counts, gain, q_w, q_b, kv_w, kv_b,
-    held, outbuf,
-    wbuf, pay, normed, partial, relay, relay_two, relay_three, meta, meta_in, bias,
+    held, outbuf, wlast, normed, partial,
+    wbuf, pay, relay, relay_two, relay_three, meta, meta_in, bias,
     ld_sem, cache_sem, send, recv, pay_send, pay_recv, meta_send, meta_recv,
     relay_send, relay_recv, two_send, two_recv, three_send, three_recv,
 ):
@@ -45,22 +50,27 @@
     xp, xym, xyp, xy2 = rank(1, 0), rank(1, 3), rank(1, 1), rank(1, 2)
     other = me + 1 - 2 * core
 
+    split = blocks - GRP
+
+    def part(first, count, start, size):
+        buf, first = (wbuf, first) if first < split else (wlast, first - split)
+        return buf.at[pl.ds(first, count), pl.ds(start, size), :]
+
     def region(r, first, count):
-        rows = pl.ds(pl.multiple_of(r * depth, 32), depth)
-        return wbuf.at[pl.ds(first, count), rows, :]
+        return part(first, count, pl.multiple_of(r * depth, 32), depth)
 
     def remote(ref, cls, g, to):
         return pltpu.make_async_remote_copy(
-            src_ref=ref, dst_ref=ref, send_sem=send, recv_sem=recv.at[cls, g],
+            src_ref=ref, dst_ref=ref, send_sem=send.at[g // (groups - 1)], recv_sem=recv.at[cls, g],
             device_id=(sec, to), device_id_type=MESH,
         )
 
-    sent = []
+    sent = [0, 0]
 
     def push(r, first, count, cls, g, to):
         copy = remote(region(r, first, count), cls, g, to)
         copy.start()
-        sent.append(count)
+        sent[g // (groups - 1)] += count
 
     def arrive(r, first, count, cls, g):
         remote(region(r, first, count), cls, g, other).wait_recv()
@@ -71,8 +81,9 @@
             src = q_w.at[:, pl.ds(j * COLS, COLS)]
         else:
             src = kv_w.at[:, pl.ds((j - q_blocks) * COLS, COLS)]
+        buf, k = (wbuf, j) if j < split else (wlast, j - split)
         rows = pl.ds(pl.multiple_of(me * depth, 32), depth)
-        copy = pltpu.make_async_copy(src, wbuf.at[j, rows, :], ld_sem.at[j])
+        copy = pltpu.make_async_copy(src, buf.at[k, rows, :], ld_sem.at[j])
         copy.start()
         loads.append(copy)
 
@@ -316,17 +327,16 @@
 
     once = jnp.where(me >= 0, 1, 0)
 
-    def product(j, start, size):
-        part = pl.ds(pl.multiple_of(start, BLK), size)
-        return jnp.dot(normed[:, part], wbuf[j, part, :], preferred_element_type=jnp.float32)
+    def product(buf, j, start, size):
+        cut = pl.ds(pl.multiple_of(start, BLK), size)
+        return jnp.dot(normed[:, cut], buf[j, cut, :], preferred_element_type=jnp.float32)
 
     def finish(j, total):
         cols = pl.ds(pl.multiple_of(j * COLS, COLS), COLS)
         outbuf[j] = (total + bias[:, cols]).astype(jnp.bfloat16)
 
     def handed(first, count, shards, cls, g):
-        whole = wbuf.at[pl.ds(first, count), pl.ds(0, shards * depth), :]
-        remote(whole, cls, g, other).wait_recv()
+        remote(part(first, count, 0, shards * depth), cls, g, other).wait_recv()
 
     def near(g):
         handed(g * GRP, GRP, 4, D_OWN, g)
@@ -338,7 +348,7 @@
         handed(g * GRP + 1, 2, 1, D_FAR, g)
 
         def one(j, carry):
-            finish(j, product(j, 0, normed.shape[1]))
+            finish(j, product(wbuf, j, 0, normed.shape[1]))
             return carry
 
         lax.fori_loop(g * GRP + 1, (g + 1) * GRP, one, 0)
@@ -348,43 +358,28 @@
         handed(a, 1, 3, D_A, g)
 
         def one(j, carry):
-            finish(j, product(j, 0, normed.shape[1]))
+            finish(j, product(wbuf, j, 0, normed.shape[1]))
             return carry
 
         lax.fori_loop(a, a + once, one, 0)
 
-    side = normed.shape[1] // 2
-    quarter = side // 2
-    mine, yours = x * side, (1 - x) * side
-    late = (((y + 2) % 4) // 2) * quarter
-    soon = quarter - late
+    side, quarter, late = quarters(x, y, normed.shape[1])
+    mine, yours, soon = x * side, (1 - x) * side, quarter - late
 
     def prepare(g):
-        a = g * GRP + 1
         near(g)
 
         def one(k, carry):
-            partial[k] = product(a + k, mine + soon, quarter) + product(a + k, yours + soon, quarter)
+            partial[k] = product(wlast, 1 + k, mine + soon, quarter) + product(wlast, 1 + k, yours + soon, quarter)
             return carry
 
         lax.fori_loop(0, GRP - 1, one, 0)
 
     def extend(g):
-        a = g * GRP + 1
         handed(g * GRP, GRP, 1, D_Y2, g)
 
         def one(k, carry):
-            partial[k] += product(a + k, mine + late, quarter)
-            return carry
-
-        lax.fori_loop(0, GRP - 1, one, 0)
-
-    def complete(g):
-        a = g * GRP + 1
-        handed(a, 2, 1, D_FAR, g)
-
-        def one(k, carry):
-            finish(a + k, partial[k] + product(a + k, yours + late, quarter))
+            partial[k] += product(wlast, 1 + k, mine + late, quarter)
             return carry
 
         lax.fori_loop(0, GRP - 1, one, 0)
@@ -459,17 +454,19 @@
     sides(4)
     sides(5)
     extend(5)
-    complete(5)
     single(4)
-    single(5)
-
-    slabs, left = divmod(sum(sent), blocks)
-    assert left == 0
-    everything = wbuf.at[:, pl.ds(0, slabs * depth), :]
-    pltpu.make_async_remote_copy(
-        src_ref=everything, dst_ref=everything, send_sem=send, recv_sem=recv.at[0, 0],
-        device_id=(sec, other), device_id_type=MESH,
-    ).wait_send()
+    handed(5 * GRP + 1, 2, 1, D_FAR, 5)
+    handed(5 * GRP, 1, 3, D_A, 5)
+
+    for k, buf in enumerate((wbuf, wlast)):
+        slabs, left = divmod(sent[k], buf.shape[0])
+        assert left == 0
+        everything = buf.at[:, pl.ds(0, slabs * depth), :]
+        pltpu.make_async_remote_copy(
+            src_ref=everything, dst_ref=everything, send_sem=send.at[k], recv_sem=recv.at[0, 0],
+            device_id=(sec, other), device_id_type=MESH,
+        ).wait_send()
+
     @pl.when(sec != last)
     def _():
         meta_copy().wait_send()
@@ -495,14 +492,32 @@
         last_hop(3).wait_send()
 
 
-def write(held, outbuf, rebuilt, queries, keys_values, sem):
+def write(held, outbuf, wlast, normed, partial, kv_b, rebuilt, queries, keys_values, tail, sem):
+    first = outbuf.shape[0]
     q_blocks = queries.shape[1] // COLS
-    copies = [pltpu.make_async_copy(held, rebuilt, sem.at[outbuf.shape[0]])]
-    for j in range(outbuf.shape[0]):
+    me = lax.axis_index("rep")
+    x, y = me // 8, (me // 2) % 4
+    side, quarter, late = quarters(x, y, normed.shape[1])
+
+    def put(src, j):
         out, k = (queries, j) if j < q_blocks else (keys_values, j - q_blocks)
-        copies.append(pltpu.make_async_copy(outbuf.at[j], out.at[:, pl.ds(k * COLS, COLS)], sem.at[j]))
+        return pltpu.make_async_copy(src, out.at[:, pl.ds(k * COLS, COLS)], sem.at[j])
+
+    copies = [pltpu.make_async_copy(held, rebuilt, sem.at[first + GRP])]
+    copies += [put(outbuf.at[j], j) for j in range(first)]
     for copy in copies:
         copy.start()
+    cut = pl.ds(pl.multiple_of((1 - x) * side + late, BLK), quarter)
+    for k in (0, 1, 2):
+        if k == 0:
+            total = jnp.dot(normed[...], wlast[k], preferred_element_type=jnp.float32)
+        else:
+            total = partial[k - 1] + jnp.dot(normed[:, cut], wlast[k, cut, :], preferred_element_type=jnp.float32)
+        at = (first + k - q_blocks) * COLS
+        tail[k] = (total + kv_b[:, at : at + COLS]).astype(jnp.bfloat16)
+        copy = put(tail.at[k], first + k)
+        copy.start()
+        copies.append(copy)
     for copy in copies:
         copy.wait()
 
@@ -521,19 +536,20 @@
     anywhere = pl.BlockSpec(memory_space=pl.ANY)
     vmem = pl.BlockSpec(memory_space=pltpu.VMEM)
     dma = pltpu.SemaphoreType.DMA
-    held, outbuf = pl.pallas_call(
+    held, outbuf, wlast, normed, partial = pl.pallas_call(
         kernel,
         out_shape=(
             pltpu.VMEM((rows, feature), jnp.bfloat16),
-            pltpu.VMEM((blocks, rows, COLS), jnp.bfloat16),
+            pltpu.VMEM((blocks - GRP, rows, COLS), jnp.bfloat16),
+            pltpu.VMEM((GRP, feature, COLS), jnp.bfloat16),
+            pltpu.VMEM((rows, feature), jnp.bfloat16),
+            pltpu.VMEM((GRP - 1, rows, COLS), jnp.float32),
         ),
         in_specs=[anywhere, anywhere, vmem, vmem, vmem, vmem, vmem, vmem, anywhere, vmem, anywhere, vmem],
-        out_specs=(vmem, vmem),
+        out_specs=(vmem,) * 5,
         scratch_shapes=[
-            pltpu.VMEM((blocks, feature, COLS), jnp.bfloat16),
+            pltpu.VMEM((blocks - GRP, feature, COLS), jnp.bfloat16),
             pltpu.VMEM((rows, feature), jnp.bfloat16),
-            pltpu.VMEM((rows, feature), jnp.bfloat16),
-            pltpu.VMEM((GRP - 1, rows, COLS), jnp.float32),
             pltpu.VMEM((BLK, feature), jnp.bfloat16),
             pltpu.VMEM((BLK, feature), jnp.bfloat16),
             pltpu.VMEM((BLK, feature), jnp.bfloat16),
@@ -542,7 +558,7 @@
             pltpu.VMEM((1, q_cols + kv_cols), jnp.float32),
             dma((blocks,)),
             dma,
-            dma,
+            dma((2,)),
             dma((CLASSES, groups)),
             dma((row_blocks,)),
             dma((row_blocks,)),
@@ -555,7 +571,7 @@
             dma,
             dma,
         ],
-        compiler_params=pltpu.CompilerParams(collective_id=0, has_side_effects=True, vmem_limit_bytes=48 * 1024 * 1024),
+        compiler_params=pltpu.CompilerParams(collective_id=0, has_side_effects=True, vmem_limit_bytes=38 * 1024 * 1024),
         name="boundary",
     )(
         cache[0], payload[0], block_ids[0], block_counts, block_scales[0], refresh_ids[0], refresh_counts,
@@ -564,12 +580,12 @@
     rebuilt, queries, keys_values = pl.pallas_call(
         write,
         out_shape=tuple(jax.ShapeDtypeStruct((rows, n), jnp.bfloat16) for n in (feature, q_cols, kv_cols)),
-        in_specs=[vmem, vmem],
+        in_specs=[vmem] * 6,
         out_specs=(anywhere, anywhere, anywhere),
-        scratch_shapes=[dma((blocks + 1,))],
-        compiler_params=pltpu.CompilerParams(vmem_limit_bytes=1024 * 1024),
+        scratch_shapes=[pltpu.VMEM((GRP, rows, COLS), jnp.bfloat16), dma((blocks + 1,))],
+        compiler_params=pltpu.CompilerParams(vmem_limit_bytes=4 * 1024 * 1024),
         name="write",
-    )(held, outbuf)
+    )(held, outbuf, wlast, normed, partial, kv_bias)
     return rebuilt[None], queries[None], keys_values[None]
 
 

time: 131 us -> 130 us (level)
  Pallas kernels: 129 us -> 127 us
    pallas_call x1, Pallas kernels: 125 us -> 124 us  [body(): pl.pallas_call(kernel, out_shape=(pltpu.VMEM((rows, feature), jnp.bfloat1...]
where the time goes in v6:
time: 130 us; the launch traced here: 129 us
  Pallas kernels  127 us (98%)
  between operations  1.95 us (2%)
    pallas_call x1, Pallas kernels, body(): pl.pallas_call(kernel, out_shape=(pltpu.VMEM((rows, feature), jnp.bfloat1...  124 us
    pallas_call x1, Pallas kernels, body(): pl.pallas_call(write, out_shape=tuple((jax.ShapeDtypeStruct((rows, n), jn...  3.61 us

profile of v6, /device:TPU:1, one launch (start us, length us, event | category | flops | bytes accessed | tf_op | source)
XLA Modules:
  0.0 129.4 jit_solution(1363536826719812938)
XLA Ops:
  1.9 0.0 copy-start
  1.9 123.9 %boundary.1 = (bf16[512,3584]{1,0:T(8,128)(2,1)S(1)}, bf16[15,512,256]{2,1,0:T(8,128)(2,1)S(1)}, bf16[3,3584,256]{2,1,0:T(8,128)(2,1)S(1)}, bf16[512,3584]{1,0:T(8,128)(2,1)S(1)}, f32[2,512,256]{2,1,0:T(8,128)S(1)}) custom-call(bf16[512,3584]{1,0:T(8,128)(2,1)} %bitcast.10, bf16[512,3584]{1,0:T(8,128)(2,1)} %bitcast.11, s32[1,2]{1,0:T(1,128)} %bitcast.14, ...), custom_call_target="tpu_custom_call" | custom-call | tf_op jit(solution)/shard_map/boundary/pallas_call | solution.py:539
  125.8 0.0 copy-done
  125.8 3.6 %write.1 = (bf16[512,3584]{1,0:T(8,128)(2,1)}, bf16[512,3584]{1,0:T(8,128)(2,1)}, bf16[512,1024]{1,0:T(8,128)(2,1)}) custom-call(bf16[512,3584]{1,0:T(8,128)(2,1)S(1)} %get-tuple-element.11.held, bf16[15,512,256]{2,1,0:T(8,128)(2,1)S(1)} %get-tuple-element.12.outbuf, bf16[3,3584,256]{2,1,0:T(8,128)(2,1)S(1)} %get-tuple-element.13.wlast, ...), custom_call_target="tpu_custom_call" | custom-call | tf_op jit(solution)/shard_map/write/pallas_call | solution.py:580
Async XLA Ops:
  1.9 123.9 %copy-start = (f32[1,1024]{1,0:T(1,128)S(1)}, f32[1,1024]{1,0:T(1,128)}, u32[]{:S(2)}) copy-start(f32[1,1024]{1,0:T(1,128)} %kv_b.3) | copy-start | bytes 12292

commit v7 on v6

--- a/solution.py
+++ b/solution.py
@@ -27,10 +27,11 @@
 
 
 def kernel(
-    cache, payload, ids, counts, scales, refresh_ids, refresh_counts, gain, q_w, q_b, kv_w, kv_b,
+    cache, payload, ids_in, counts_in, scales_in, refresh_ids_in, refresh_counts_in, gain_in, q_w, q_b, kv_w, kv_b,
     held, outbuf, wlast, normed, partial,
     wbuf, pay, relay, relay_two, relay_three, meta, meta_in, bias,
     ld_sem, cache_sem, send, recv, pay_send, pay_recv, meta_send, meta_recv,
+    ids, counts, scales, refresh_ids, refresh_counts, gain, small_sem,
     relay_send, relay_recv, two_send, two_recv, three_send, three_recv,
 ):
     sec = lax.axis_index("section")
@@ -74,6 +75,25 @@
 
     def arrive(r, first, count, cls, g):
         remote(region(r, first, count), cls, g, other).wait_recv()
+
+    last = lax.axis_size("section") - 1
+    half = (last + 1) // 2
+    barrier = pltpu.get_barrier_semaphore()
+
+    def greet(to_sec, to_rep):
+        pl.semaphore_signal(barrier, inc=1, device_id=(to_sec, to_rep), device_id_type=MESH)
+
+    for r in (ym, yp, xp, other):
+        greet(sec, r)
+    expected = 4
+    links = [(s + 1, s, me) for s in range(last)]
+    links += [(0, half - 1, me), (last, half - 1, xp), (half, half - 1, xp), (half, last, xp), (half, 0, xp)]
+    for receiver, sender, r in links:
+        @pl.when(sec == receiver)
+        def _():
+            greet(sender, r)
+
+        expected = expected + jnp.where(sec == sender, 1, 0)
 
     loads = []
     for j in range(blocks):
@@ -87,6 +107,25 @@
         copy.start()
         loads.append(copy)
 
+    q_cols = q_w.shape[1]
+    small = [
+        pltpu.make_async_copy(src, dst, small_sem.at[i])
+        for i, (src, dst) in enumerate(
+            (
+                (ids_in, ids), (counts_in, counts), (scales_in, scales), (refresh_ids_in, refresh_ids),
+                (refresh_counts_in, refresh_counts), (gain_in, gain),
+                (q_b, bias.at[:, pl.ds(0, q_cols)]), (kv_b, bias.at[:, pl.ds(q_cols, kv_w.shape[1])]),
+            )
+        )
+    ]
+    for copy in small:
+        copy.start()
+    load_cache = pltpu.make_async_copy(cache, held, cache_sem)
+    load_cache.start()
+
+    for copy in small:
+        copy.wait()
+
     lane = lax.broadcasted_iota(jnp.int32, (1, BLK), 1)
 
     def two(v):
@@ -99,27 +138,6 @@
     meta[4:5, :] = jnp.broadcast_to(counts[...], (1, BLK))
     meta[5:8, :] = jnp.zeros((3, BLK), jnp.int32)
 
-    load_cache = pltpu.make_async_copy(cache, held, cache_sem)
-    load_cache.start()
-
-    last = lax.axis_size("section") - 1
-    half = (last + 1) // 2
-    barrier = pltpu.get_barrier_semaphore()
-
-    def greet(to_sec, to_rep):
-        pl.semaphore_signal(barrier, inc=1, device_id=(to_sec, to_rep), device_id_type=MESH)
-
-    for r in (ym, yp, xp, other):
-        greet(sec, r)
-    expected = 4
-    links = [(s + 1, s, me) for s in range(last)]
-    links += [(0, half - 1, me), (last, half - 1, xp), (half, half - 1, xp), (half, last, xp), (half, 0, xp)]
-    for receiver, sender, r in links:
-        @pl.when(sec == receiver)
-        def _():
-            greet(sender, r)
-
-        expected = expected + jnp.where(sec == sender, 1, 0)
     pl.semaphore_wait(barrier, expected)
 
     def block(ref, b):
@@ -226,9 +244,6 @@
                 first_hop(1).start()
 
         push(me, g * GRP, GRP, D_OWN, g, other)
-
-    bias[:, : q_w.shape[1]] = q_b[...]
-    bias[:, q_w.shape[1] :] = kv_b[...]
 
     def level1(g):
         a = g * GRP
@@ -342,26 +357,25 @@
         handed(g * GRP, GRP, 4, D_OWN, g)
         handed(g * GRP + 1, 2, 2, D_SIDE, g)
 
-    def pair(g):
+    def pair_ready(g):
         near(g)
         handed(g * GRP, GRP, 1, D_Y2, g)
         handed(g * GRP + 1, 2, 1, D_FAR, g)
 
+    def multiply(first, count):
         def one(j, carry):
             finish(j, product(wbuf, j, 0, normed.shape[1]))
             return carry
 
-        lax.fori_loop(g * GRP + 1, (g + 1) * GRP, one, 0)
+        lax.fori_loop(first, first + count * once, one, 0)
+
+    def pair(g):
+        pair_ready(g)
+        multiply(g * GRP + 1, 2)
 
     def single(g):
-        a = g * GRP
-        handed(a, 1, 3, D_A, g)
-
-        def one(j, carry):
-            finish(j, product(wbuf, j, 0, normed.shape[1]))
-            return carry
-
-        lax.fori_loop(a, a + once, one, 0)
+        handed(g * GRP, 1, 3, D_A, g)
+        multiply(g * GRP, 1)
 
     side, quarter, late = quarters(x, y, normed.shape[1])
     mine, yours, soon = x * side, (1 - x) * side, quarter - late
@@ -444,16 +458,18 @@
     opposite_a(5)
     sides(3)
     single(2)
-    pair(4)
+    pair_ready(4)
+    multiply(4 * GRP + 1, 1)
     level2_up(5)
+    multiply(4 * GRP + 2, 1)
     level2_down(5)
+    single(3)
     opposite(5)
-    single(3)
     prepare(5)
     far(5)
     sides(4)
+    extend(5)
     sides(5)
-    extend(5)
     single(4)
     handed(5 * GRP + 1, 2, 1, D_FAR, 5)
     handed(5 * GRP, 1, 3, D_A, 5)
@@ -545,7 +561,7 @@
             pltpu.VMEM((rows, feature), jnp.bfloat16),
             pltpu.VMEM((GRP - 1, rows, COLS), jnp.float32),
         ),
-        in_specs=[anywhere, anywhere, vmem, vmem, vmem, vmem, vmem, vmem, anywhere, vmem, anywhere, vmem],
+        in_specs=[anywhere] * 12,
         out_specs=(vmem,) * 5,
         scratch_shapes=[
             pltpu.VMEM((blocks - GRP, feature, COLS), jnp.bfloat16),
@@ -564,6 +580,13 @@
             dma((row_blocks,)),
             dma,
             dma,
+            pltpu.VMEM(block_ids.shape[1:], jnp.int32),
+            pltpu.VMEM(block_counts.shape, jnp.int32),
+            pltpu.VMEM(block_scales.shape[1:], jnp.int32),
+            pltpu.VMEM(refresh_ids.shape[1:], jnp.int32),
+            pltpu.VMEM(refresh_counts.shape, jnp.int32),
+            pltpu.VMEM(norm_gain.shape, jnp.float32),
+            dma((8,)),
             dma,
             dma,
             dma,

time: 130 us -> 128 us (0.985)
    pallas_call x1, Pallas kernels: 124 us -> 122 us  [body(): pl.pallas_call(kernel, out_shape=(pltpu.VMEM((rows, feature), jnp.bfloat1...]
where the time goes in v7:
time: 128 us
  Pallas kernels  126 us (98%)
  between operations  1.95 us (2%)
    pallas_call x1, Pallas kernels, body(): pl.pallas_call(kernel, out_shape=(pltpu.VMEM((rows, feature), jnp.bfloat1...  122 us
    pallas_call x1, Pallas kernels, body(): pl.pallas_call(write, out_shape=tuple((jax.ShapeDtypeStruct((rows, n), jn...  3.61 us

profile of v7, /device:TPU:1, one launch (start us, length us, event | category | flops | bytes accessed | tf_op | source)
XLA Modules:
  0.0 128.0 jit_solution(11477288802565687488)
XLA Ops:
  1.9 0.0 copy-start
  1.9 122.5 %boundary.1 = (bf16[512,3584]{1,0:T(8,128)(2,1)S(1)}, bf16[15,512,256]{2,1,0:T(8,128)(2,1)S(1)}, bf16[3,3584,256]{2,1,0:T(8,128)(2,1)S(1)}, bf16[512,3584]{1,0:T(8,128)(2,1)S(1)}, f32[2,512,256]{2,1,0:T(8,128)S(1)}) custom-call(bf16[512,3584]{1,0:T(8,128)(2,1)} %bitcast.10, bf16[512,3584]{1,0:T(8,128)(2,1)} %bitcast.11, s32[1,2]{1,0:T(1,128)} %bitcast.14, ...), custom_call_target="tpu_custom_call" | custom-call | tf_op jit(solution)/shard_map/boundary/pallas_call | solution.py:555
  124.4 0.0 copy-done
  124.4 3.6 %write.1 = (bf16[512,3584]{1,0:T(8,128)(2,1)}, bf16[512,3584]{1,0:T(8,128)(2,1)}, bf16[512,1024]{1,0:T(8,128)(2,1)}) custom-call(bf16[512,3584]{1,0:T(8,128)(2,1)S(1)} %get-tuple-element.11.held, bf16[15,512,256]{2,1,0:T(8,128)(2,1)S(1)} %get-tuple-element.12.outbuf, bf16[3,3584,256]{2,1,0:T(8,128)(2,1)S(1)} %get-tuple-element.13.wlast, ...), custom_call_target="tpu_custom_call" | custom-call | tf_op jit(solution)/shard_map/write/pallas_call | solution.py:603
Async XLA Ops:
  1.9 122.5 %copy-start = (f32[1,1024]{1,0:T(1,128)S(1)}, f32[1,1024]{1,0:T(1,128)}, u32[]{:S(2)}) copy-start(f32[1,1024]{1,0:T(1,128)} %kv_b.3) | copy-start | bytes 12292

commit v8 on v7

--- a/solution.py
+++ b/solution.py
@@ -519,7 +519,10 @@
         out, k = (queries, j) if j < q_blocks else (keys_values, j - q_blocks)
         return pltpu.make_async_copy(src, out.at[:, pl.ds(k * COLS, COLS)], sem.at[j])
 
-    copies = [pltpu.make_async_copy(held, rebuilt, sem.at[first + GRP])]
+    copies = []
+    for b in range(held.shape[0] // BLK):
+        rows = pl.ds(b * BLK, BLK)
+        copies.append(pltpu.make_async_copy(held.at[rows, :], rebuilt.at[rows, :], sem.at[first + GRP + b]))
     copies += [put(outbuf.at[j], j) for j in range(first)]
     for copy in copies:
         copy.start()
@@ -605,7 +608,7 @@
         out_shape=tuple(jax.ShapeDtypeStruct((rows, n), jnp.bfloat16) for n in (feature, q_cols, kv_cols)),
         in_specs=[vmem] * 6,
         out_specs=(anywhere, anywhere, anywhere),
-        scratch_shapes=[pltpu.VMEM((GRP, rows, COLS), jnp.bfloat16), dma((blocks + 1,))],
+        scratch_shapes=[pltpu.VMEM((GRP, rows, COLS), jnp.bfloat16), dma((blocks + row_blocks,))],
         compiler_params=pltpu.CompilerParams(vmem_limit_bytes=4 * 1024 * 1024),
         name="write",
     )(held, outbuf, wlast, normed, partial, kv_bias)

time: 128 us -> 129 us (level)
  no operation moved by 1% of the time
where the time goes in v8:
time: 129 us
  Pallas kernels  127 us (98%)
  between operations  1.95 us (2%)
    pallas_call x1, Pallas kernels, body(): pl.pallas_call(kernel, out_shape=(pltpu.VMEM((rows, feature), jnp.bfloat1...  122 us
    pallas_call x1, Pallas kernels, body(): pl.pallas_call(write, out_shape=tuple((jax.ShapeDtypeStruct((rows, n), jn...  4.24 us

profile of v8, /device:TPU:1, one launch (start us, length us, event | category | flops | bytes accessed | tf_op | source)
XLA Modules:
  0.0 128.7 jit_solution(5968878761129796222)
XLA Ops:
  1.9 0.0 copy-start
  1.9 122.5 %boundary.1 = (bf16[512,3584]{1,0:T(8,128)(2,1)S(1)}, bf16[15,512,256]{2,1,0:T(8,128)(2,1)S(1)}, bf16[3,3584,256]{2,1,0:T(8,128)(2,1)S(1)}, bf16[512,3584]{1,0:T(8,128)(2,1)S(1)}, f32[2,512,256]{2,1,0:T(8,128)S(1)}) custom-call(bf16[512,3584]{1,0:T(8,128)(2,1)} %bitcast.10, bf16[512,3584]{1,0:T(8,128)(2,1)} %bitcast.11, s32[1,2]{1,0:T(1,128)} %bitcast.14, ...), custom_call_target="tpu_custom_call" | custom-call | tf_op jit(solution)/shard_map/boundary/pallas_call | solution.py:558
  124.4 0.0 copy-done
  124.4 4.2 %write.1 = (bf16[512,3584]{1,0:T(8,128)(2,1)}, bf16[512,3584]{1,0:T(8,128)(2,1)}, bf16[512,1024]{1,0:T(8,128)(2,1)}) custom-call(bf16[512,3584]{1,0:T(8,128)(2,1)S(1)} %get-tuple-element.11.held, bf16[15,512,256]{2,1,0:T(8,128)(2,1)S(1)} %get-tuple-element.12.outbuf, bf16[3,3584,256]{2,1,0:T(8,128)(2,1)S(1)} %get-tuple-element.13.wlast, ...), custom_call_target="tpu_custom_call" | custom-call | tf_op jit(solution)/shard_map/write/pallas_call | solution.py:606
Async XLA Ops:
  1.9 122.5 %copy-start = (f32[1,1024]{1,0:T(1,128)S(1)}, f32[1,1024]{1,0:T(1,128)}, u32[]{:S(2)}) copy-start(f32[1,1024]{1,0:T(1,128)} %kv_b.3) | copy-start | bytes 12292
